TPU v7x, 256 devices: a whole 4x4x8 slice. The times are simulated.
256 devices in a mesh: row: 32 (over z_hi, x, y), col: 8 (over z_lo, core).
Axes of the slice: x: 4, y: 4, z: 8 (z_hi: 2, z_lo: 4; z = z_hi * 4 + z_lo), core: 2. Of those that a mesh axis runs over, the one named last changes fastest.
Arguments:
- query_proj: bfloat16 [768, 768, 128], P('row', 'col'), may hold values from -8 to 8
- key_proj: bfloat16 [768, 768, 128], P('row', 'col'), may hold values from -8 to 8
- value_proj: bfloat16 [768, 768, 128], P('row', 'col'), may hold values from -6 to 6
- pair_bias: bfloat16 [4, 768, 768], P(None, 'col', 'row'), may hold values from -9 to 9
- pair_mask: int32 [768, 768], P('row', 'col'), may hold values 0 or 1
- grad_out: bfloat16 [768, 768, 128], P('row', 'col'), may hold values from -18 to 18
Outputs:
- grad_query: bfloat16 [768, 768, 128], P('row', 'col')
- grad_key: bfloat16 [768, 768, 128], P('row', 'col')
- grad_value: bfloat16 [768, 768, 128], P('row', 'col')
- grad_bias: float32 [4, 768, 768], P(None, 'col', 'row')
All inputs are finite; a program needn't handle non-finite values. No bound on the sum of `pair_mask` on one device may be relied on, other than what follows from the above.
Results may differ from a plain program's by a relative error of at most 0.0096.
Values may be sent and summed in bfloat16 or wider, within the bound.
A program may use at most 128 MiB of HBM per device.

v0:
```python
import math

import jax
import jax.numpy as jnp
from jax import lax
from jax.sharding import Mesh
from jax.sharding import PartitionSpec as P

HEADS = 4
HEAD_DIM = 32
COL = ("col_0", "col_1")


def in_order(blocks, dim):
    lengths = list(blocks.shape[1:])
    lengths[dim] *= blocks.shape[0]
    return jnp.moveaxis(blocks, 0, dim).reshape(lengths)


def copy_for_each(value, axis):
    copies = jnp.broadcast_to(value, (lax.axis_size(axis), *value.shape))
    return lax.all_to_all(copies, axis, split_axis=0, concat_axis=0, tiled=True)


def gathered_copies(value, axis, dim):
    return in_order(copy_for_each(value, axis), dim)


def sum_in_order(blocks, axes, turns):
    inside = blocks.shape[1:]
    blocks = blocks.reshape(*(lax.axis_size(a) for a in axes), *inside)
    blocks = jnp.moveaxis(blocks, turns, range(len(axes))).reshape(-1, *inside)
    for k in turns:
        blocks = lax.psum_scatter(blocks, axes[k], scatter_dimension=0, tiled=True)
    return blocks[0]


def in_blocks(value, dim, length):
    lengths = value.shape
    blocks = value.reshape(*lengths[:dim], length, lengths[dim] // length, *lengths[dim + 1 :])
    return jnp.moveaxis(blocks, dim, 0)


def summed_rows(value, axes, turns, dim):
    length = lax.axis_size(axes)
    return sum_in_order(in_blocks(value, dim, length), axes, turns)


def summed_on_arrival(value, axis, dim):
    blocks = in_blocks(value, dim, lax.axis_size(axis))
    arrived = lax.all_to_all(blocks, axis, split_axis=0, concat_axis=0, tiled=True)
    return arrived.sum(axis=0)


def block_grads(queries, keys_all, values_all, grads, mask_all, bias_full):
    block_rows, query_count, channel_count = queries.shape
    key_count = keys_all.shape[1]
    scale = 1.0 / math.sqrt(HEAD_DIM)
    query_heads = queries.reshape(block_rows, query_count, HEADS, HEAD_DIM)
    key_heads = keys_all.reshape(block_rows, key_count, HEADS, HEAD_DIM)
    value_heads = values_all.reshape(block_rows, key_count, HEADS, HEAD_DIM)
    grad_heads = grads.reshape(block_rows, query_count, HEADS, HEAD_DIM)
    masked = 1000000000.0 * (mask_all.astype(jnp.float32) - 1.0)
    scores = (
        jnp.einsum("bjhd,bkhd->bhjk", query_heads, key_heads, preferred_element_type=jnp.float32)
        * scale
    )
    scores = scores + bias_full.astype(jnp.float32)[None] + masked[:, None, None, :]
    top_score = jnp.max(scores, axis=-1, keepdims=True)
    weights = jnp.exp(scores - top_score)
    attn_probs = weights / jnp.sum(weights, axis=-1, keepdims=True)
    attn_low = attn_probs.astype(jnp.bfloat16)
    attended = jnp.einsum(
        "bhjk,bkhd->bjhd", attn_low, value_heads, preferred_element_type=jnp.float32
    )
    row_delta = jnp.sum(grad_heads.astype(jnp.float32) * attended, axis=-1)
    grad_probs = jnp.einsum(
        "bjhd,bkhd->bhjk", grad_heads, value_heads, preferred_element_type=jnp.float32
    )
    grad_scores = attn_probs * (grad_probs - jnp.transpose(row_delta, (0, 2, 1))[..., None])
    scores_low = grad_scores.astype(jnp.bfloat16)
    grad_queries = (
        jnp.einsum("bhjk,bkhd->bjhd", scores_low, key_heads, preferred_element_type=jnp.float32)
        * scale
    )
    grad_keys = (
        jnp.einsum("bhjk,bjhd->bkhd", scores_low, query_heads, preferred_element_type=jnp.float32)
        * scale
    )
    grad_values = jnp.einsum(
        "bhjk,bjhd->bkhd", attn_low, grad_heads, preferred_element_type=jnp.float32
    )
    bias_grad = jnp.sum(grad_scores, axis=0)
    return (
        grad_queries.reshape(block_rows, query_count, channel_count),
        grad_keys.reshape(block_rows, key_count, channel_count),
        grad_values.reshape(block_rows, key_count, channel_count),
        bias_grad,
    )


def all_blocks(queries, keys_all, values_all, grads, mask_all, bias_full):
    row_count, query_count, channel_count = queries.shape
    key_count = keys_all.shape[1]
    block_rows = 1
    while (
        block_rows * 2 <= row_count
        and row_count % (block_rows * 2) == 0
        and (block_rows * query_count < 512)
    ):
        block_rows = block_rows * 2
    steps_count = row_count // block_rows

    def split_rows(array):
        return array.reshape((steps_count, block_rows) + array.shape[1:])

    def one_block(bias_sum, pieces):
        grad_queries, grad_keys, grad_values, bias_grad = block_grads(
            pieces[0], pieces[1], pieces[2], pieces[3], pieces[4], bias_full
        )
        return (bias_sum + bias_grad, (grad_queries, grad_keys, grad_values))

    start_sum = jnp.zeros((HEADS, query_count, key_count), jnp.float32)
    bias_sum, stacked = lax.scan(
        one_block,
        start_sum,
        (
            split_rows(queries),
            split_rows(keys_all),
            split_rows(values_all),
            split_rows(grads),
            split_rows(mask_all),
        ),
    )
    return (
        stacked[0].reshape(row_count, query_count, channel_count),
        stacked[1].reshape(row_count, key_count, channel_count),
        stacked[2].reshape(row_count, key_count, channel_count),
        bias_sum,
    )


def local(query_proj, key_proj, value_proj, pair_bias, pair_mask, grad_out):
    bias_rows = gathered_copies(pair_bias, "row", 2)
    mask_low = pair_mask.astype(jnp.bfloat16)
    local_tiles = (
        lax.all_to_all(query_proj, COL, split_axis=0, concat_axis=1, tiled=True),
        lax.all_to_all(key_proj, COL, split_axis=0, concat_axis=1, tiled=True),
        lax.all_to_all(value_proj, COL, split_axis=0, concat_axis=1, tiled=True),
        lax.all_to_all(grad_out, COL, split_axis=0, concat_axis=1, tiled=True),
        lax.all_to_all(mask_low, COL, split_axis=0, concat_axis=1, tiled=True),
    )
    bias_full = lax.all_gather(bias_rows, COL, axis=1, tiled=True)
    grad_queries, grad_keys, grad_values, bias_whole = all_blocks(
        local_tiles[0], local_tiles[1], local_tiles[2], local_tiles[3], local_tiles[4], bias_full
    )
    grad_query, grad_key, grad_value = (
        lax.all_to_all(
            grad_queries.astype(jnp.bfloat16), COL, split_axis=1, concat_axis=0, tiled=True
        ),
        lax.all_to_all(
            grad_keys.astype(jnp.bfloat16), COL, split_axis=1, concat_axis=0, tiled=True
        ),
        lax.all_to_all(
            grad_values.astype(jnp.bfloat16), COL, split_axis=1, concat_axis=0, tiled=True
        ),
    )
    bias_part = summed_rows(bias_whole, COL, (1, 0), 1)
    grad_bias = summed_on_arrival(bias_part, "row", 2)
    return (grad_query, grad_key, grad_value, grad_bias)


def solution(mesh):
    torus = Mesh(mesh.devices.reshape(mesh.shape["row"], 4, 2), ("row", "col_0", "col_1"))
    placed = (
        P("row", COL, None),
        P("row", COL, None),
        P("row", COL, None),
        P(None, COL, "row"),
        P("row", COL),
        P("row", COL, None),
    )
    return jax.shard_map(
        local,
        mesh=torus,
        in_specs=placed,
        out_specs=(
            P("row", COL, None),
            P("row", COL, None),
            P("row", COL, None),
            P(None, COL, "row"),
        ),
        check_vma=False,
    )
```

profile of v0, /device:TPU:38, one launch (start us, length us, event | category | flops | bytes accessed | tf_op | source)
XLA Modules:
  0.0 576.0 jit_solution(17604812634602663810)
XLA Ops:
  8.1 38.3 %all_to_all.140 = bf16[32,4,96,24]{2,3,1,0:T(8,128)(2,1)S(1)} all-to-all(bf16[32,4,96,24]{2,3,1,0:T(8,128)(2,1)S(1)} %broadcast_in_dim.31), channel_id=1, replica_groups=mesh['row'=32,'col_0'=4,'col_1'=2] {'row'}, dimensions={0} | all-to-all | bytes 1179648 | tf_op jit(solution)/shard_map/all_to_all | solution.py:22
  46.4 1.2 copy.101
  48.3 7.7 %all_to_all.141 = bf16[8,3,96]{2,1,0:T(4,128)(2,1)S(1)} all-to-all(bf16[8,3,96]{2,1,0:T(4,128)(2,1)S(1)} %all_to_all.108), channel_id=1, replica_groups=mesh['row'=32,'col_0'=4,'col_1'=2] {'col_0','col_1'}, dimensions={0} | all-to-all | bytes 9216 | tf_op jit(solution)/shard_map/all_to_all | solution.py:151
  56.1 29.2 %all_to_all.142 = bf16[24,96,128]{2,1,0:T(8,128)(2,1)S(1)} all-to-all(bf16[24,96,128]{2,1,0:T(8,128)(2,1)} %param.8), channel_id=1, replica_groups=mesh['row'=32,'col_0'=4,'col_1'=2] {'col_0','col_1'}, dimensions={0} | all-to-all | bytes 1179648 | tf_op jit(solution)/shard_map/all_to_all | solution.py:147
  85.3 30.0 %all_to_all.143 = bf16[24,96,128]{2,1,0:T(8,128)(2,1)S(1)} all-to-all(bf16[24,96,128]{2,1,0:T(8,128)(2,1)} %param.9), channel_id=1, replica_groups=mesh['row'=32,'col_0'=4,'col_1'=2] {'col_0','col_1'}, dimensions={0} | all-to-all | bytes 1179648 | tf_op jit(solution)/shard_map/all_to_all | solution.py:148
  115.3 23.4 %all_to_all.144 = bf16[24,96,128]{2,1,0:T(8,128)(2,1)S(1)} all-to-all(bf16[24,96,128]{2,1,0:T(8,128)(2,1)} %param.10), channel_id=1, replica_groups=mesh['row'=32,'col_0'=4,'col_1'=2] {'col_0','col_1'}, dimensions={0} | all-to-all | bytes 1179648 | tf_op jit(solution)/shard_map/all_to_all | solution.py:149
  138.7 5.1 all-to-all-start.4
  144.1 13.0 %all-to-all-done.4 = bf16[24,96,128]{2,1,0:T(8,128)(2,1)S(1)} async-done(((bf16[24,96,128]{2,1,0:T(8,128)(2,1)}), bf16[24,96,128]{2,1,0:T(8,128)(2,1)S(1)}, u32[]{:S(2)}, u32[]{:S(2)}) %all-to-all-start.4) | async-done | bytes 589856 | tf_op jit(solution)/shard_map/all_to_all | solution.py:150
  158.0 8.5 %copy.107 = bf16[4,768,768]{1,2,0:T(8,128)(2,1)} copy(bf16[4,768,768]{2,0,1:T(4,128)(2,1)} %all-gather.2.cloned.1.call-done) | data formatting | bytes 9437184
  166.4 181.6 %while.19 = (s32[]{:T(128)}, f32[4,768,768]{1,2,0:T(8,128)}, bf16[3,1,768,128]{3,0,2,1:T(4,128)(2,1)}, bf16[3,1,768,128]{3,0,2,1:T(4,128)(2,1)}, bf16[3,1,768,12...) while((s32[]{:T(128)}, f32[4,768,768]{1,2,0:T(8,128)}, ...), condition=%wide.region_4.5_spmd.clone, body=%wide.region_0.4_spmd.clone.sunk | while | flops 939687936 | bytes 88149664 | solution.py:124
  166.5 1.0 constant_dynamic-slice_fusion.6
  168.1 7.3 %fusion.60 = (f32[4,768]{1,0:T(4,128)S(1)}, f32[4,768,768]{1,2,0:T(8,128)}) fusion(bf16[4,768,768]{1,2,0:T(8,128)(2,1)} %get-tuple-element.376, f32[768]{0:T(1024)S(1)} %multiply_reduce_fusion.2, bf16[768,4,32]{0,2,1:T(8,128)(2,1)S(1)} %bitcast.151, bf16[768,4,32]{0,2,1:T(8,128)(2,1)S(1)} %bitcast.148), kind=kOutput, calls=%fused_computation.26.clone.1 | convolution fusion | flops 165151488 | bytes 14564352 | tf_op jit(solution)/shard_map/while/body/eval_jaxpr/sub | solution.py:70
  175.4 4.4 fusion.61
  180.8 1.5 fusion.65
  182.7 10.4 %dynamic_update_slice.27 = bf16[3,1,768,128]{3,0,2,1:T(4,128)(2,1)} dynamic-update-slice(bf16[3,1,768,128]{3,0,2,1:T(4,128)(2,1)} %get-tuple-element.360, bf16[1,1,768,128]{3,0,2,1:T(2,128)(2,1)S(1)} %copy.153, s32[]{:T(128)S(6)} %copy.162, s32[]{:T(128)} %constant.55.clone.1..sunk, s32[]{:T(128)} %constant.55.clone.1..sunk, s32[]{:T(128)} %constant.55.clone.1..sunk) | dynamic-update-slice | bytes 393220 | tf_op jit(solution)/shard_map/while/body/jit(dynamic_update_index_in_dim)/dynamic_update_slice | solution.py:124
  193.1 7.1 %select_add_fusion.2 = (f32[4,768,768]{1,2,0:T(8,128)}, bf16[4,768,768]{1,2,0:T(8,128)(2,1)S(1)}) fusion(f32[4,768,768]{1,2,0:T(8,128)} %get-tuple-element.357, pred[]{:T(512)S(6)} %compare.3, f32[4,768]{1,0:T(4,128)S(1)} %bitcast.173, bf16[768,4,32]{0,2,1:T(8,128)(2,1)S(1)} %bitcast.143, bf16[768,4,32]{0,2,1:T(8,128)(2,1)S(1)} %bitcast.147, ...), kind=kOutput, calls=%fused_computation.1.clone.1 | convolution fusion | flops 165150720 | bytes 33447936 | tf_op jit(solution)/shard_map/while/body/eval_jaxpr/bjhd,bkhd->bhjk/dot_general | solution.py:77
  200.2 1.5 fusion.64
  203.5 10.4 %dynamic_update_slice.25 = bf16[3,1,768,128]{3,0,2,1:T(4,128)(2,1)} dynamic-update-slice(bf16[3,1,768,128]{3,0,2,1:T(4,128)(2,1)} %get-tuple-element.358, bf16[1,1,768,128]{3,0,2,1:T(2,128)(2,1)S(1)} %copy.151, s32[]{:T(128)S(6)} %copy.162, s32[]{:T(128)} %constant.55.clone.1..sunk, s32[]{:T(128)} %constant.55.clone.1..sunk, s32[]{:T(128)} %constant.55.clone.1..sunk) | dynamic-update-slice | bytes 393220 | tf_op jit(solution)/shard_map/while/body/jit(dynamic_update_index_in_dim)/dynamic_update_slice | solution.py:124
  213.9 10.4 %dynamic_update_slice.26 = bf16[3,1,768,128]{3,0,2,1:T(4,128)(2,1)} dynamic-update-slice(bf16[3,1,768,128]{3,0,2,1:T(4,128)(2,1)} %get-tuple-element.359, bf16[1,1,768,128]{3,0,2,1:T(2,128)(2,1)S(1)} %copy.152, s32[]{:T(128)S(6)} %copy.162, s32[]{:T(128)} %constant.55.clone.1..sunk, s32[]{:T(128)} %constant.55.clone.1..sunk, s32[]{:T(128)} %constant.55.clone.1..sunk) | dynamic-update-slice | bytes 393220 | tf_op jit(solution)/shard_map/while/body/jit(dynamic_update_index_in_dim)/dynamic_update_slice | solution.py:124
  224.4 1.0 constant_dynamic-slice_fusion.6
  226.0 7.3 %fusion.60 = (f32[4,768]{1,0:T(4,128)S(1)}, f32[4,768,768]{1,2,0:T(8,128)}) fusion(bf16[4,768,768]{1,2,0:T(8,128)(2,1)} %get-tuple-element.376, f32[768]{0:T(1024)S(1)} %multiply_reduce_fusion.2, bf16[768,4,32]{0,2,1:T(8,128)(2,1)S(1)} %bitcast.151, bf16[768,4,32]{0,2,1:T(8,128)(2,1)S(1)} %bitcast.148), kind=kOutput, calls=%fused_computation.26.clone.1 | convolution fusion | flops 165151488 | bytes 14564352 | tf_op jit(solution)/shard_map/while/body/eval_jaxpr/sub | solution.py:70
  233.3 4.4 fusion.61
  238.7 1.5 fusion.65
  240.6 10.4 %dynamic_update_slice.27 = bf16[3,1,768,128]{3,0,2,1:T(4,128)(2,1)} dynamic-update-slice(bf16[3,1,768,128]{3,0,2,1:T(4,128)(2,1)} %get-tuple-element.360, bf16[1,1,768,128]{3,0,2,1:T(2,128)(2,1)S(1)} %copy.153, s32[]{:T(128)S(6)} %copy.162, s32[]{:T(128)} %constant.55.clone.1..sunk, s32[]{:T(128)} %constant.55.clone.1..sunk, s32[]{:T(128)} %constant.55.clone.1..sunk) | dynamic-update-slice | bytes 393220 | tf_op jit(solution)/shard_map/while/body/jit(dynamic_update_index_in_dim)/dynamic_update_slice | solution.py:124
  251.1 11.0 %select_add_fusion.2 = (f32[4,768,768]{1,2,0:T(8,128)}, bf16[4,768,768]{1,2,0:T(8,128)(2,1)S(1)}) fusion(f32[4,768,768]{1,2,0:T(8,128)} %get-tuple-element.357, pred[]{:T(512)S(6)} %compare.3, f32[4,768]{1,0:T(4,128)S(1)} %bitcast.173, bf16[768,4,32]{0,2,1:T(8,128)(2,1)S(1)} %bitcast.143, bf16[768,4,32]{0,2,1:T(8,128)(2,1)S(1)} %bitcast.147, ...), kind=kOutput, calls=%fused_computation.1.clone.1 | convolution fusion | flops 165150720 | bytes 33447936 | tf_op jit(solution)/shard_map/while/body/eval_jaxpr/bjhd,bkhd->bhjk/dot_general | solution.py:77
  262.1 1.5 fusion.64
  265.3 10.4 %dynamic_update_slice.25 = bf16[3,1,768,128]{3,0,2,1:T(4,128)(2,1)} dynamic-update-slice(bf16[3,1,768,128]{3,0,2,1:T(4,128)(2,1)} %get-tuple-element.358, bf16[1,1,768,128]{3,0,2,1:T(2,128)(2,1)S(1)} %copy.151, s32[]{:T(128)S(6)} %copy.162, s32[]{:T(128)} %constant.55.clone.1..sunk, s32[]{:T(128)} %constant.55.clone.1..sunk, s32[]{:T(128)} %constant.55.clone.1..sunk) | dynamic-update-slice | bytes 393220 | tf_op jit(solution)/shard_map/while/body/jit(dynamic_update_index_in_dim)/dynamic_update_slice | solution.py:124
  275.8 10.4 %dynamic_update_slice.26 = bf16[3,1,768,128]{3,0,2,1:T(4,128)(2,1)} dynamic-update-slice(bf16[3,1,768,128]{3,0,2,1:T(4,128)(2,1)} %get-tuple-element.359, bf16[1,1,768,128]{3,0,2,1:T(2,128)(2,1)S(1)} %copy.152, s32[]{:T(128)S(6)} %copy.162, s32[]{:T(128)} %constant.55.clone.1..sunk, s32[]{:T(128)} %constant.55.clone.1..sunk, s32[]{:T(128)} %constant.55.clone.1..sunk) | dynamic-update-slice | bytes 393220 | tf_op jit(solution)/shard_map/while/body/jit(dynamic_update_index_in_dim)/dynamic_update_slice | solution.py:124
  287.8 7.3 %fusion.60 = (f32[4,768]{1,0:T(4,128)S(1)}, f32[4,768,768]{1,2,0:T(8,128)}) fusion(bf16[4,768,768]{1,2,0:T(8,128)(2,1)} %get-tuple-element.376, f32[768]{0:T(1024)S(1)} %multiply_reduce_fusion.2, bf16[768,4,32]{0,2,1:T(8,128)(2,1)S(1)} %bitcast.151, bf16[768,4,32]{0,2,1:T(8,128)(2,1)S(1)} %bitcast.148), kind=kOutput, calls=%fused_computation.26.clone.1 | convolution fusion | flops 165151488 | bytes 14564352 | tf_op jit(solution)/shard_map/while/body/eval_jaxpr/sub | solution.py:70
  295.2 4.4 fusion.61
  300.6 1.5 fusion.65
  302.5 10.4 %dynamic_update_slice.27 = bf16[3,1,768,128]{3,0,2,1:T(4,128)(2,1)} dynamic-update-slice(bf16[3,1,768,128]{3,0,2,1:T(4,128)(2,1)} %get-tuple-element.360, bf16[1,1,768,128]{3,0,2,1:T(2,128)(2,1)S(1)} %copy.153, s32[]{:T(128)S(6)} %copy.162, s32[]{:T(128)} %constant.55.clone.1..sunk, s32[]{:T(128)} %constant.55.clone.1..sunk, s32[]{:T(128)} %constant.55.clone.1..sunk) | dynamic-update-slice | bytes 393220 | tf_op jit(solution)/shard_map/while/body/jit(dynamic_update_index_in_dim)/dynamic_update_slice | solution.py:124
  312.9 11.0 %select_add_fusion.2 = (f32[4,768,768]{1,2,0:T(8,128)}, bf16[4,768,768]{1,2,0:T(8,128)(2,1)S(1)}) fusion(f32[4,768,768]{1,2,0:T(8,128)} %get-tuple-element.357, pred[]{:T(512)S(6)} %compare.3, f32[4,768]{1,0:T(4,128)S(1)} %bitcast.173, bf16[768,4,32]{0,2,1:T(8,128)(2,1)S(1)} %bitcast.143, bf16[768,4,32]{0,2,1:T(8,128)(2,1)S(1)} %bitcast.147, ...), kind=kOutput, calls=%fused_computation.1.clone.1 | convolution fusion | flops 165150720 | bytes 33447936 | tf_op jit(solution)/shard_map/while/body/eval_jaxpr/bjhd,bkhd->bhjk/dot_general | solution.py:77
  323.9 1.5 fusion.64
  327.2 10.4 %dynamic_update_slice.25 = bf16[3,1,768,128]{3,0,2,1:T(4,128)(2,1)} dynamic-update-slice(bf16[3,1,768,128]{3,0,2,1:T(4,128)(2,1)} %get-tuple-element.358, bf16[1,1,768,128]{3,0,2,1:T(2,128)(2,1)S(1)} %copy.151, s32[]{:T(128)S(6)} %copy.162, s32[]{:T(128)} %constant.55.clone.1..sunk, s32[]{:T(128)} %constant.55.clone.1..sunk, s32[]{:T(128)} %constant.55.clone.1..sunk) | dynamic-update-slice | bytes 393220 | tf_op jit(solution)/shard_map/while/body/jit(dynamic_update_index_in_dim)/dynamic_update_slice | solution.py:124
  337.6 10.4 %dynamic_update_slice.26 = bf16[3,1,768,128]{3,0,2,1:T(4,128)(2,1)} dynamic-update-slice(bf16[3,1,768,128]{3,0,2,1:T(4,128)(2,1)} %get-tuple-element.359, bf16[1,1,768,128]{3,0,2,1:T(2,128)(2,1)S(1)} %copy.152, s32[]{:T(128)S(6)} %copy.162, s32[]{:T(128)} %constant.55.clone.1..sunk, s32[]{:T(128)} %constant.55.clone.1..sunk, s32[]{:T(128)} %constant.55.clone.1..sunk) | dynamic-update-slice | bytes 393220 | tf_op jit(solution)/shard_map/while/body/jit(dynamic_update_index_in_dim)/dynamic_update_slice | solution.py:124
  348.0 9.6 %copy.120 = f32[4,768,768]{2,1,0:T(8,128)} copy(f32[4,768,768]{1,2,0:T(8,128)} %get-tuple-element.147) | data formatting | bytes 18874368 | tf_op jit(solution)/shard_map/while | solution.py:124
  357.6 8.3 %copy.121 = f32[4,2,4,96,768]{4,3,2,0,1:T(8,128)} copy(f32[4,2,4,96,768]{4,3,1,0,2:T(8,128)} %bitcast.145) | data formatting | bytes 18874368 | tf_op jit(solution)/shard_map/reshape | solution.py:31
  366.0 21.3 %reduce-scatter.3.cloned.1.call-done = f32[4,4,96,768]{3,2,1,0:T(8,128)} async-done(((f32[8,4,96,768]{3,2,1,0:T(8,128)}), f32[4,4,96,768]{3,2,1,0:T(8,128)}) %reduce-scatter.3.cloned.1.call-update) | async-done | bytes 4718608 | tf_op jit(solution)/shard_map/reduce_scatter | solution.py:34
  387.3 34.3 %all_to_all.145 = bf16[3,768,128]{2,0,1:T(4,128)(2,1)} all-to-all(bf16[3,768,128]{2,0,1:T(4,128)(2,1)S(1)} %bitcast.168), channel_id=1, replica_groups=mesh['row'=32,'col_0'=4,'col_1'=2] {'col_0','col_1'}, dimensions={1} | all-to-all | bytes 1179648 | tf_op jit(solution)/shard_map/all_to_all | solution.py:164
  421.6 48.5 %all_to_all.146 = bf16[3,768,128]{2,0,1:T(4,128)(2,1)S(1)} all-to-all(bf16[3,768,128]{2,0,1:T(4,128)(2,1)S(1)} %bitcast.169), channel_id=1, replica_groups=mesh['row'=32,'col_0'=4,'col_1'=2] {'col_0','col_1'}, dimensions={1} | all-to-all | bytes 1179648 | tf_op jit(solution)/shard_map/all_to_all | solution.py:158
  470.0 6.7 %all-to-all-start.7 = ((bf16[3,768,128]{2,0,1:T(4,128)(2,1)}), bf16[3,768,128]{2,0,1:T(4,128)(2,1)S(1)}, u32[]{:S(2)}, u32[]{:S(2)}) async-start(bf16[3,768,128]{2,0,1:T(4,128)(2,1)} %bitcast.83), calls=%async_computation.7 | async-start | bytes 1572864 | tf_op jit(solution)/shard_map/all_to_all | solution.py:161
  476.8 46.2 %reduce-scatter.5.cloned.1.call-done = f32[1,4,96,768]{3,2,1,0:T(8,128)} async-done(((f32[4,4,96,768]{3,2,1,0:T(8,128)}), f32[1,4,96,768]{3,2,1,0:T(8,128)}) %reduce-scatter.5.cloned.1.call-update) | async-done | bytes 1179664 | tf_op jit(solution)/shard_map/reduce_scatter | solution.py:34
  522.9 1.7 copy.122
  524.7 1.4 copy.123
  526.0 11.0 %all-to-all-start.9 = ((f32[32,4,96,24]{2,3,1,0:T(8,128)}), f32[32,4,96,24]{2,3,1,0:T(8,128)S(1)}, u32[]{:S(2)}, u32[]{:S(2)}) async-start(f32[32,4,96,24]{2,3,1,0:T(8,128)} %copy.123), calls=%async_computation.11 | async-start | bytes 3145728 | tf_op jit(solution)/shard_map/all_to_all | solution.py:51
  537.0 1.2 copy.118
  541.0 27.8 %all-to-all-done.9 = f32[32,4,96,24]{2,3,1,0:T(8,128)S(1)} async-done(((f32[32,4,96,24]{2,3,1,0:T(8,128)}), f32[32,4,96,24]{2,3,1,0:T(8,128)S(1)}, u32[]{:S(2)}, u32[]{:S(2)}) %all-to-all-start.9) | async-done | bytes 1179680 | tf_op jit(solution)/shard_map/all_to_all | solution.py:51
  (66 shorter events, 18.6 us)
Async XLA Ops:
  7.2 150.8 %all-gather.2.cloned.1.call-start = ((), (), s32[]{:S(2)}) async-start(), calls=%async_computation.12 | async-start | bytes 5308416 | tf_op jit(solution)/shard_map/all_gather | solution.py:153
  138.7 18.4 %all-to-all-start.4 = ((bf16[24,96,128]{2,1,0:T(8,128)(2,1)}), bf16[24,96,128]{2,1,0:T(8,128)(2,1)S(1)}, u32[]{:S(2)}, u32[]{:S(2)}) async-start(bf16[24,96,128]{2,1,0:T(8,128)(2,1)} %param.13), calls=%async_computation.4 | async-start | bytes 1179648 | tf_op jit(solution)/shard_map/all_to_all | solution.py:150
  143.8 243.5 %reduce-scatter.3.cloned.1.call-start = ((), (), s32[]{:S(2)}) async-start(), calls=%async_computation.13 | async-start | bytes 14155776 | tf_op jit(solution)/shard_map/reduce_scatter | solution.py:34
  365.9 21.4 %copy-start = (bf16[3,1,768,128]{3,0,2,1:T(4,128)(2,1)S(1)}, bf16[3,1,768,128]{3,0,2,1:T(4,128)(2,1)}, u32[]{:S(2)}) copy-start(bf16[3,1,768,128]{3,0,2,1:T(4,128)(2,1)} %get-tuple-element.146) | copy-start | bytes 1769476
  365.9 55.7 %copy-start.1 = (bf16[3,1,768,128]{3,0,2,1:T(4,128)(2,1)S(1)}, bf16[3,1,768,128]{3,0,2,1:T(4,128)(2,1)}, u32[]{:S(2)}) copy-start(bf16[3,1,768,128]{3,0,2,1:T(4,128)(2,1)} %get-tuple-element.144) | copy-start | bytes 1769476
  366.0 157.0 %reduce-scatter.5.cloned.1.call-start = ((), (), s32[]{:S(2)}) async-start(), calls=%async_computation.14 | async-start | bytes 5898240 | tf_op jit(solution)/shard_map/reduce_scatter | solution.py:34
  470.0 56.0 %all-to-all-start.7 = ((bf16[3,768,128]{2,0,1:T(4,128)(2,1)}), bf16[3,768,128]{2,0,1:T(4,128)(2,1)S(1)}, u32[]{:S(2)}, u32[]{:S(2)}) async-start(bf16[3,768,128]{2,0,1:T(4,128)(2,1)} %bitcast.83), calls=%async_computation.7 | async-start | bytes 1572864 | tf_op jit(solution)/shard_map/all_to_all | solution.py:161
  526.0 42.7 %all-to-all-start.9 = ((f32[32,4,96,24]{2,3,1,0:T(8,128)}), f32[32,4,96,24]{2,3,1,0:T(8,128)S(1)}, u32[]{:S(2)}, u32[]{:S(2)}) async-start(f32[32,4,96,24]{2,3,1,0:T(8,128)} %copy.123), calls=%async_computation.11 | async-start | bytes 3145728 | tf_op jit(solution)/shard_map/all_to_all | solution.py:51
Sparse Core Ops, SparseCore 0:
  47.7 76.9 all-gather.1
  366.1 21.1 reduce-scatter.2
  389.8 133.0 reduce-scatter.4
where the time goes:
time: 583 us; the launch traced here: 576 us
  blocking collectives  211 us (36%)
  local copies, waits for them, and re-layouts  139 us (24%)
  waiting for transfers between devices  108 us (19%)
  matrix products  65.4 us (11%)
  starting transfers between devices  22.9 us (4%)
  other arithmetic  14.9 us (3%)
  between operations  13.8 us (2%)
    dynamic_update_slice x18, local copies, waits for them, and re-layouts, all_blocks(): lax.scan(one_block, start_sum, (split_rows(queries), split_rows(keys_all)...  97.8 us
    reduce_scatter x2, waiting for transfers between devices, sum_in_order(): blocks = lax.psum_scatter(blocks, axes[k], scatter_dimension=0, tiled=True)  67.4 us
    all_to_all x1, blocking collectives, local(): lax.all_to_all(grad_queries.astype(jnp.bfloat16), COL, split_axis=1, conc...  48.5 us
    all_to_all x1, blocking collectives, copy_for_each(): return lax.all_to_all(copies, axis, split_axis=0, concat_axis=0, tiled=True)  38.3 us
    all_to_all x1, blocking collectives, local(): lax.all_to_all(grad_values.astype(jnp.bfloat16), COL, split_axis=1, conca...  34.3 us
    all_to_all x1, blocking collectives, local(): lax.all_to_all(key_proj, COL, split_axis=0, concat_axis=1, tiled=True)  30 us
    all_to_all x1, blocking collectives, local(): lax.all_to_all(query_proj, COL, split_axis=0, concat_axis=1, tiled=True)  29.2 us
    dot_general x3, matrix products, block_grads(): jnp.einsum('bjhd,bkhd->bhjk', grad_heads, value_heads, preferred_element_...  29.2 us
  transfers between devices with their start and end apart: 6, of which 4 were waited for; matrix products, arithmetic and copies ran while one was open for 2% of the time, Pallas kernels for 0%

commit v1 on v0

v1 whole, which is shorter than its diff:
```python
import functools
import math

import jax
import jax.numpy as jnp
from jax import lax
from jax.experimental import pallas as pl
from jax.experimental.pallas import tpu as pltpu
from jax.sharding import Mesh
from jax.sharding import PartitionSpec as P

HEADS = 4
HEAD_DIM = 32
SCALE = 1.0 / math.sqrt(HEAD_DIM)
ROW = ("zh", "x", "y")
COL = ("zl", "core")
MESH = pl.DeviceIdType.MESH
LANES = 128
CHUNK = 256
F32 = jnp.float32
BF16 = jnp.bfloat16


def dot(a, b, dims):
    return lax.dot_general(a, b, (dims, ((), ())), preferred_element_type=F32)


def kernel(
    zs,
    cs,
    send_ref,
    mask_ref,
    bias_ref,
    out_ref,
    gb_ref,
    ab,
    biasf,
    mrecv,
    maskt,
    maskf,
    kq,
    vg,
    kt,
    vk,
    dqt,
    obuf,
    mask_ssem,
    mask_rsem,
    in_ssem,
    in_rsem,
    in_lsem,
    out_ssem,
    out_rsem,
    out_lsem,
):
    n = ab.shape[2]
    width = send_ref.shape[3]
    rows = ab.shape[0]
    groups = rows // 2
    peers = zs * cs
    tiles, _, tile, _ = bias_ref.shape
    zl, core = lax.axis_index("zl"), lax.axis_index("core")
    me = zl * cs + core

    def peer_of(offset):
        other = lax.rem(me + offset, peers)
        return other, other // cs, lax.rem(other, cs)

    def target(z, c):
        return {"zl": z, "core": c}

    barrier = pltpu.get_barrier_semaphore()
    for offset in range(1, peers):
        _, z, c = peer_of(offset)
        pl.semaphore_signal(barrier, inc=1, device_id=target(z, c), device_id_type=MESH)
    pl.semaphore_wait(barrier, peers - 1)

    my_columns = pl.ds(pl.multiple_of(me * width, width), width)

    def mask_copy(offset):
        _, z, c = peer_of(offset)
        return pltpu.make_async_remote_copy(
            src_ref=mask_ref.at[z],
            dst_ref=mrecv.at[me],
            send_sem=mask_ssem.at[offset],
            recv_sem=mask_rsem.at[offset],
            device_id=target(z, c),
            device_id_type=MESH,
        )

    def in_copy(group, offset):
        _, z, c = peer_of(offset)
        return pltpu.make_async_remote_copy(
            src_ref=send_ref.at[c, pl.ds(z * rows + group * 2, 2)],
            dst_ref=ab.at[pl.ds(group * 2, 2), :, my_columns],
            send_sem=in_ssem.at[group, offset],
            recv_sem=in_rsem.at[group, offset],
            device_id=target(z, c),
            device_id_type=MESH,
        )

    def in_local(group):
        return pltpu.make_async_copy(
            send_ref.at[core, pl.ds(zl * rows + group * 2, 2)],
            ab.at[pl.ds(group * 2, 2), :, my_columns],
            in_lsem.at[group],
        )

    def out_copy(group, offset):
        other, z, c = peer_of(offset)
        return pltpu.make_async_remote_copy(
            src_ref=obuf.at[group, :, pl.ds(pl.multiple_of(other * width, width), width)],
            dst_ref=out_ref.at[core, zl * groups + group],
            send_sem=out_ssem.at[group, offset],
            recv_sem=out_rsem.at[group, offset],
            device_id=target(z, c),
            device_id_type=MESH,
        )

    def out_local(group):
        return pltpu.make_async_copy(
            obuf.at[group, :, my_columns],
            out_ref.at[core, zl * groups + group],
            out_lsem.at[group],
        )

    for offset in range(1, peers):
        mask_copy(offset).start()
    mask_local = pltpu.make_async_copy(mask_ref.at[zl], mrecv.at[me], mask_ssem.at[0])
    mask_local.start()
    for group in range(groups):
        for offset in range(1, peers):
            in_copy(group, offset).start()
        in_local(group).start()

    def widen(r, carry):
        for h in range(2):
            biasf[h, pl.ds(pl.multiple_of(r * tile, 8), tile), :] = bias_ref[r, h].astype(F32)
        return carry

    lax.fori_loop(0, tiles, widen, 0)
    gb_ref[...] = jnp.zeros_like(gb_ref)

    mask_local.wait()
    for offset in range(1, peers):
        mask_copy(offset).wait()
    for s in range(peers):
        maskt[s * width : (s + 1) * width, :] = jnp.transpose(mrecv[s])[:width]
    for i in range(rows):
        maskf[i] = jnp.broadcast_to(maskt[:, i : i + 1], (n, LANES))

    lane_head = lax.broadcasted_iota(jnp.int32, (1, LANES), 1) // HEAD_DIM

    def one_group(group, carry):
        in_local(group).wait()
        for offset in range(1, peers):
            in_copy(group, offset).wait()

        def one_row(r, carry):
            i = group * 2 + r
            a = ab[i, 0].astype(F32)
            b = ab[i, 1].astype(F32)
            ar = pltpu.roll(a, 64, 1)
            br = pltpu.roll(b, 64, 1)
            for h in range(2):
                kq[h] = jnp.where(lane_head == h, ar, 0.0).astype(BF16)
                kq[2 + h] = jnp.where(lane_head == 2 + h, ar, 0.0).astype(BF16)
                vg[h] = jnp.where(lane_head == h, br, 0.0).astype(BF16)
                vg[2 + h] = jnp.where(lane_head == h, b, 0.0).astype(BF16)
            kt[...] = jnp.transpose(ar).astype(BF16)
            vk[...] = jnp.zeros_like(vk)

            def one_chunk(t, carry):
                h, ch = t // (n // CHUNK), lax.rem(t, n // CHUNK)
                cols = pl.ds(pl.multiple_of(ch * CHUNK, CHUNK), CHUNK)
                s = dot(kq[h], ab[i, 0, cols, :], ((1,), (1,)))
                dp = dot(vg[h], ab[i, 1, cols, :], ((1,), (1,)))
                m128 = maskf[i]
                mask = jnp.concatenate([m128] * (CHUNK // LANES), axis=1)
                s = (s * SCALE + biasf[h, :, cols]) + mask
                top = jnp.max(s, axis=0, keepdims=True)
                e = jnp.exp(s - top)
                inverse = 1.0 / jnp.sum(e, axis=0, keepdims=True)
                delta = jnp.sum(e * dp, axis=0, keepdims=True) * inverse
                p = e * inverse
                ds = p * (dp - delta)
                low = ds.astype(BF16)
                gb_ref[:, h, :, cols] += ds.reshape(tiles, tile, CHUNK)
                vk[...] += dot(p.astype(BF16), vg[2 + h, cols, :], ((1,), (0,))) + dot(
                    low, kq[2 + h, cols, :], ((1,), (0,))
                )
                head_rows = kt[pl.ds(pl.multiple_of(h * HEAD_DIM, HEAD_DIM), HEAD_DIM), :]
                at = pl.multiple_of(r * 64 + h * HEAD_DIM, HEAD_DIM)
                dqt[pl.ds(at, HEAD_DIM), cols] = dot(head_rows, low, ((1,), (0,)))
                return carry

            lax.fori_loop(0, 2 * (n // CHUNK), one_chunk, 0)
            obuf[group, r] = (vk[...] * jnp.where(lane_head < 2, 1.0, SCALE)).astype(BF16)
            return carry

        lax.fori_loop(0, 2, one_row, 0)
        obuf[group, 2] = (jnp.transpose(dqt[...]) * SCALE).astype(BF16)
        for offset in range(1, peers):
            out_copy(group, offset).start()
        out_local(group).start()
        return carry

    lax.fori_loop(0, groups, one_group, 0)

    def drain(group, carry):
        out_local(group).wait()
        for offset in range(1, peers):
            out_copy(group, offset).wait()
        return carry

    lax.fori_loop(0, groups, drain, 0)


def attention(zs, cs, send, mask, bias):
    width = send.shape[3]
    n = zs * cs * width
    rows = send.shape[1] // zs
    groups = rows // 2
    peers = zs * cs
    tiles, _, tile, _ = bias.shape
    any_spec = pl.BlockSpec(memory_space=pl.ANY)
    vmem_spec = pl.BlockSpec(memory_space=pltpu.VMEM)
    dma = pltpu.SemaphoreType.DMA
    return pl.pallas_call(
        functools.partial(kernel, zs, cs),
        out_shape=(
            jax.ShapeDtypeStruct((cs, zs * groups, 3, width, LANES), BF16),
            jax.ShapeDtypeStruct((tiles, 2, tile, n), F32),
        ),
        in_specs=[any_spec, any_spec, vmem_spec],
        out_specs=(any_spec, vmem_spec),
        scratch_shapes=[
            pltpu.VMEM((rows, 2, n, LANES), BF16),
            pltpu.VMEM((2, n, n), F32),
            pltpu.VMEM((peers, 8, LANES), F32),
            pltpu.VMEM((n, 8), F32),
            pltpu.VMEM((rows, n, LANES), F32),
            pltpu.VMEM((4, n, LANES), BF16),
            pltpu.VMEM((4, n, LANES), BF16),
            pltpu.VMEM((LANES, n), BF16),
            pltpu.VMEM((n, LANES), F32),
            pltpu.VMEM((LANES, n), F32),
            pltpu.VMEM((groups, 3, n, LANES), BF16),
            dma((peers,)),
            dma((peers,)),
            dma((groups, peers)),
            dma((groups, peers)),
            dma((groups,)),
            dma((groups, peers)),
            dma((groups, peers)),
            dma((groups,)),
        ],
        compiler_params=pltpu.CompilerParams(
            collective_id=0, has_side_effects=True, vmem_limit_bytes=56 * 1024 * 1024
        ),
        cost_estimate=pl.CostEstimate(
            flops=10 * rows * 2 * n * n * LANES, bytes_accessed=32 * 1024 * 1024, transcendentals=0
        ),
        name="attention_backward",
    )(send, mask, bias)


def local(zs, cs, query_proj, key_proj, value_proj, pair_bias, pair_mask, grad_out):
    rows, width, _ = query_proj.shape
    core = lax.axis_index("core")
    half = HEADS // 2 * HEAD_DIM

    bias = jnp.transpose(pair_bias, (0, 2, 1))
    bias = lax.all_gather(bias, COL, axis=2, tiled=True)
    bias = lax.dynamic_slice_in_dim(bias, core * 2, 2, 0)
    bias = lax.all_gather(bias, ROW, axis=0, tiled=False)

    def pack(a, b):
        return jnp.stack(
            [jnp.concatenate([a[..., c * half : (c + 1) * half], b[..., c * half : (c + 1) * half]], -1) for c in range(cs)]
        )

    send = jnp.stack([pack(query_proj, key_proj), pack(grad_out, value_proj)], 2)
    mask = 1000000000.0 * (pair_mask.astype(F32) - 1.0)
    per_chip = rows // zs
    mask = jnp.pad(mask.reshape(zs, per_chip, width), ((0, 0), (0, 8 - per_chip), (0, LANES - width)))

    out, gb = attention(zs, cs, send, mask, bias)

    gb = lax.psum_scatter(gb, ROW, scatter_dimension=0, tiled=False)
    tile = gb.shape[1]
    gb = gb.reshape(2, tile, zs * cs, width).transpose(2, 0, 1, 3)
    gb = lax.all_to_all(gb, COL, split_axis=0, concat_axis=0, tiled=True)
    gb = gb.reshape(zs, cs, 2, tile, width).sum(axis=0).reshape(HEADS, tile, width)
    grad_bias = jnp.transpose(gb, (0, 2, 1))

    def rejoin(pieces):
        return jnp.concatenate([pieces[c] for c in range(cs)], axis=-1)

    value_key = out[:, :, :2].reshape(cs, rows, width, LANES)
    grad_value = rejoin(value_key[..., :half])
    grad_key = rejoin(value_key[..., half:])
    pairs = out[:, :, 2]
    pairs = jnp.stack([pairs[..., :half], pairs[..., half:]], axis=2).reshape(cs, rows, width, half)
    grad_query = rejoin(pairs)
    return grad_query, grad_key, grad_value, grad_bias


def solution(mesh):
    rows = mesh.shape["row"]
    shape = (2, 4, 4, 4, 2) if rows == 32 else (1, 1, rows, 4, 2)
    torus = Mesh(mesh.devices.reshape(shape), ROW + COL)
    pair = P(ROW, COL, None)
    tile = P(None, COL, ROW)
    return jax.shard_map(
        functools.partial(local, 4, 2),
        mesh=torus,
        in_specs=(pair, pair, pair, tile, P(ROW, COL), pair),
        out_specs=(pair, pair, pair, tile),
        check_vma=False,
    )
```

time: 583 us -> 504 us (0.86)
  the two profiles are of different devices: /device:TPU:38 before, /device:TPU:1 now
where the time goes in v1:
time: 504 us; the launch traced here: 503 us
  waiting for transfers between devices  341 us (68%)
  Pallas kernels  101 us (20%)
  blocking collectives  18.4 us (4%)
  between operations  14.2 us (3%)
  local copies, waits for them, and re-layouts  13.4 us (3%)
  other arithmetic  8.52 us (2%)
  starting transfers between devices  7.02 us (1%)
    reduce_scatter x1, waiting for transfers between devices, local(): gb = lax.psum_scatter(gb, ROW, scatter_dimension=0, tiled=False)  257 us
    pallas_call x1, Pallas kernels, attention(): pl.pallas_call(functools.partial(kernel, zs, cs), out_shape=(jax.ShapeDty...  101 us
    all_gather x1, waiting for transfers between devices, local(): bias = lax.all_gather(bias, ROW, axis=0, tiled=False)  81.5 us
    all_gather x1, blocking collectives, local(): bias = lax.all_gather(bias, COL, axis=2, tiled=True)  18.4 us
  transfers between devices with their start and end apart: 3, of which 3 were waited for; matrix products, arithmetic and copies ran while one was open for 2% of the time, Pallas kernels for 0%

profile of v1, /device:TPU:1, one launch (start us, length us, event | category | flops | bytes accessed | tf_op | source)
XLA Modules:
  0.0 503.4 jit_solution(1769872761977357922)
XLA Ops:
  7.2 0.0 copy-start.6
  7.2 0.0 all-gather.3.cloned.1.call-start
  7.2 0.9 copy.20
  8.1 0.0 copy-start
  8.1 18.4 %all_gather.9 = bf16[4,24,768]{1,0,2:T(4,128)(2,1)S(1)} all-gather(bf16[4,24,96]{1,0,2:T(4,128)(2,1)S(1)} %bitcast.43), channel_id=1, replica_groups=mesh['zh'=2,'x'=4,'y'=4,'zl'=4,'core'=2] {'zl','core'}, dimensions={2}, use_global_device_ids=true | all-gather | bytes 165888 | tf_op jit(solution)/shard_map/all_gather | solution.py:274
  26.5 0.4 constant_dynamic-slice_fusion
  26.9 0.9 copy.21
  27.8 0.0 all-gather.3.cloned.1.call-update
  27.8 0.0 reduce-scatter.2.cloned.1.call-start
  27.9 0.0 copy-done.6
  27.9 0.6 pad.4.mask_ref
  28.5 0.0 copy-done
  28.5 0.2 fusion.1
  28.8 0.8 copy-done.1
  29.6 0.2 fusion.2
  29.8 0.7 maximum_bitcast_fusion.2
  30.5 0.0 copy-start.2
  30.5 0.1 maximum_bitcast_fusion
  30.6 0.9 copy-done.2
  31.6 0.2 fusion.4
  31.8 0.8 copy-done.3
  32.6 0.2 fusion.3
  32.9 0.7 maximum_bitcast_fusion.4
  33.5 0.1 maximum_bitcast_fusion.1
  33.6 1.7 pad_maximum_fusion.send_ref
  35.3 81.5 %all-gather.3.cloned.1.call-done = bf16[64,24,768]{2,1,0:T(8,128)(2,1)} async-done(((bf16[2,24,768]{2,1,0:T(8,128)(2,1)}), bf16[64,24,768]{2,1,0:T(8,128)(2,1)}) %all-gather.3.cloned.1.call-update) | async-done | bytes 2359312 | tf_op jit(solution)/shard_map/all_gather | solution.py:276
  116.8 101.1 %attention_backward.1 = (bf16[2,12,3,96,128]{4,3,2,1,0:T(8,128)(2,1)}, f32[32,2,24,768]{3,2,1,0:T(8,128)}) custom-call(bf16[2,24,2,96,128]{4,3,2,1,0:T(8,128)(2,1)} %pad_maximum_fusion.send_ref, f32[4,8,128]{2,1,0:T(8,128)} %pad.4.mask_ref, bf16[32,2,24,768]{3,2,1,0:T(8,128)(2,1)} %bitcast.45), custom_call_target="tpu_custom_call" | custom-call | flops 9059696640 | bytes 33554432 | tf_op jit(solution)/shard_map/attention_backward/pallas_call | solution.py:229
  217.9 0.0 copy-start.4
  217.9 0.0 reduce-scatter.2.cloned.1.call-update
  218.0 1.4 copy-done.4
  219.4 0.1 slice.75
  219.6 0.2 slice_bitcast_fusion.5
  219.8 0.2 fusion
  220.1 1.0 copy.22
  221.1 1.0 copy.23
  222.0 0.4 slice_bitcast_fusion.1
  222.5 0.0 copy-start.5
  222.5 257.2 %reduce-scatter.2.cloned.1.call-done = f32[1,2,24,768]{3,2,1,0:T(8,128)} async-done(((f32[32,2,24,768]{3,2,1,0:T(8,128)}), f32[1,2,24,768]{3,2,1,0:T(8,128)}) %reduce-scatter.2.cloned.1.call-update) | async-done | bytes 147472 | tf_op jit(solution)/shard_map/reduce_scatter | solution.py:290
  479.7 1.0 reshape_reduce_scatter.3
  480.7 0.7 copy.30
  481.5 6.9 %all-to-all-start = ((f32[8,2,24,96]{3,2,1,0:T(8,128)}), f32[8,2,24,96]{3,2,1,0:T(8,128)}, u32[]{:S(2)}, u32[]{:S(2)}) async-start(f32[8,2,24,96]{3,2,1,0:T(8,128)} %bitcast.39), calls=%async_computation.1 | async-start | bytes 393216 | tf_op jit(solution)/shard_map/all_to_all | solution.py:293
  488.4 0.0 copy-done.5
  488.4 1.2 pad_maximum_fusion.1
  489.6 1.1 copy.27
  490.7 1.1 pad_maximum_fusion.4
  491.8 1.1 pad_maximum_fusion.3
  493.0 2.1 all-to-all-done
  495.0 1.6 reduce_sum.9
  (5 shorter events, 0.1 us)
Async XLA Ops:
  7.2 20.7 %copy-start.6 = (s32[24,96]{1,0:T(8,128)S(1)}, s32[24,96]{1,0:T(8,128)}, u32[]{:S(2)}) copy-start(s32[24,96]{1,0:T(8,128)} %param.10) | copy-start | bytes 27652
  7.2 109.6 %all-gather.3.cloned.1.call-start = ((), (), s32[]{:S(2)}) async-start(), calls=%async_computation.3 | async-start | bytes 2433024 | tf_op jit(solution)/shard_map/all_gather | solution.py:276
  8.1 20.4 %copy-start = (bf16[24,96,128]{2,1,0:T(8,128)(2,1)S(1)}, bf16[24,96,128]{2,1,0:T(8,128)(2,1)}, u32[]{:S(2)}) copy-start(bf16[24,96,128]{2,1,0:T(8,128)(2,1)} %param.6) | copy-start | bytes 1769476
  27.8 451.9 %reduce-scatter.2.cloned.1.call-start = ((), (), s32[]{:S(2)}) async-start(), calls=%async_computation.2 | async-start | bytes 4866048 | tf_op jit(solution)/shard_map/reduce_scatter | solution.py:290
  28.5 1.1 copy-start.1
  30.5 1.1 copy-start.2
  31.5 1.1 copy-start.3
  217.9 1.5 copy-start.4
  222.5 265.9 %copy-start.5 = (bf16[1,12,2,96,64]{3,4,2,1,0:T(8,128)(2,1)S(1)}, bf16[1,12,2,96,64]{3,4,2,1,0:T(8,128)(2,1)}, u32[]{:S(2)}) copy-start(bf16[1,12,2,96,64]{3,4,2,1,0:T(8,128)(2,1)} %copy.22) | copy-start | bytes 884740
  481.5 13.6 %all-to-all-start = ((f32[8,2,24,96]{3,2,1,0:T(8,128)}), f32[8,2,24,96]{3,2,1,0:T(8,128)}, u32[]{:S(2)}, u32[]{:S(2)}) async-start(f32[8,2,24,96]{3,2,1,0:T(8,128)} %bitcast.39), calls=%async_computation.1 | async-start | bytes 393216 | tf_op jit(solution)/shard_map/all_to_all | solution.py:293
Sparse Core Ops, SparseCore 0:
  27.9 88.8 all-gather.2
  218.1 261.5 reduce-scatter.1

commit v2 on v1

v2 whole, which is shorter than its diff:
```python
import functools
import math

import jax
import jax.numpy as jnp
from jax import lax
from jax.experimental import pallas as pl
from jax.experimental.pallas import tpu as pltpu
from jax.sharding import Mesh
from jax.sharding import PartitionSpec as P

HEADS = 4
HEAD_DIM = 32
SCALE = 1.0 / math.sqrt(HEAD_DIM)
ROW = ("zh", "x", "y")
COL = ("zl", "core")
MESH = pl.DeviceIdType.MESH
LANES = 128
CHUNK = 256
F32 = jnp.float32
BF16 = jnp.bfloat16


def dot(a, b, dims):
    return lax.dot_general(a, b, (dims, ((), ())), preferred_element_type=F32)


def kernel(
    dims,
    send_ref,
    mask_ref,
    tile_ref,
    out_ref,
    gout_ref,
    ab,
    biasb,
    biasf,
    gb,
    mrecv,
    maskt,
    maskf,
    kq,
    vg,
    kt,
    vk,
    dqt,
    obuf,
    trecv,
    first_s,
    first_r,
    second_s,
    second_r,
    partial,
    third_s,
    third_r,
    fourth_s,
    fourth_r,
    last_s,
    last_r,
    mask_sem,
    in_sem,
    in_lsem,
    out_sem,
    out_lsem,
    tile_sem,
    gather_sem,
    sum_sem,
    last_sem,
):
    zhs, zls, cs = dims
    n = ab.shape[2]
    width = send_ref.shape[3]
    tile = tile_ref.shape[2]
    rows = ab.shape[0]
    groups = rows // 2
    peers = zls * cs
    ring = zhs * peers
    chunk = min(CHUNK, n)
    chunks = n // chunk
    zh, zl, core = lax.axis_index("zh"), lax.axis_index("zl"), lax.axis_index("core")
    place = {"x": lax.axis_index("x"), "y": lax.axis_index("y")}
    me = zl * cs + core
    spot = zh * peers + me

    def remote(src, dst, sem, device):
        return pltpu.make_async_remote_copy(
            src_ref=src,
            dst_ref=dst,
            send_sem=sem.at[0],
            recv_sem=sem.at[1],
            device_id=device,
            device_id_type=MESH,
        )

    def peer_of(offset):
        other = lax.rem(me + offset, peers)
        return other, other // cs, lax.rem(other, cs)

    def ring_of(offset):
        other = lax.rem(spot + offset, ring)
        return other // peers, lax.rem(other, peers) // cs, lax.rem(other, cs)

    def ring_target(offset):
        h, z, c = ring_of(offset)
        return {"zh": h, "zl": z, "core": c}

    def step(axis, by):
        return lax.rem(place[axis] + by, 4)

    barrier = pltpu.get_barrier_semaphore()
    for offset in range(1, ring):
        pl.semaphore_signal(barrier, inc=1, device_id=ring_target(offset), device_id_type=MESH)
    for axis in ("x", "y"):
        for by in (1, 3):
            pl.semaphore_signal(barrier, inc=1, device_id={axis: step(axis, by)}, device_id_type=MESH)
    pl.semaphore_wait(barrier, ring - 1 + 4)

    def columns_of(c):
        return pl.ds(pl.multiple_of(c * width, width), width)

    def tile_copy(offset):
        _, _, c = ring_of(offset)
        return remote(tile_ref.at[c], trecv.at[spot], tile_sem.at[offset], ring_target(offset))

    def mask_copy(offset):
        _, z, c = peer_of(offset)
        return remote(mask_ref.at[z], mrecv.at[me], mask_sem.at[offset], {"zl": z, "core": c})

    def in_copy(group, offset):
        _, z, c = peer_of(offset)
        return remote(
            send_ref.at[c, pl.ds(z * rows + group * 2, 2)],
            ab.at[pl.ds(group * 2, 2), :, columns_of(me)],
            in_sem.at[group, offset],
            {"zl": z, "core": c},
        )

    def in_local(group):
        return pltpu.make_async_copy(
            send_ref.at[core, pl.ds(zl * rows + group * 2, 2)],
            ab.at[pl.ds(group * 2, 2), :, columns_of(me)],
            in_lsem.at[group],
        )

    def out_copy(group, offset):
        other, z, c = peer_of(offset)
        return remote(
            obuf.at[group, :, columns_of(other)],
            out_ref.at[core, zl * groups + group],
            out_sem.at[group, offset],
            {"zl": z, "core": c},
        )

    def out_local(group):
        return pltpu.make_async_copy(
            obuf.at[group, :, columns_of(me)],
            out_ref.at[core, zl * groups + group],
            out_lsem.at[group],
        )

    orders = (("x", "y"), ("y", "x"))

    def block(h, phase, index, half):
        axis = orders[h][phase]
        other = "y" if axis == "x" else "x"
        at = {axis: index, other: place[other] if phase == 0 else slice(None)}
        return biasb.at[h, slice(None) if half is None else half, at["x"], at["y"]]

    def gather_copy(h, phase, hop, way):
        axis = orders[h][phase]
        by = (1, 3)[way]
        if hop == 0:
            ref = block(h, phase, place[axis], None)
        else:
            ref = block(h, phase, step(axis, 4 - by), way)
        return remote(ref, ref, gather_sem.at[h, phase, hop, way], {axis: step(axis, by)})

    tile_local = pltpu.make_async_copy(tile_ref.at[core], trecv.at[spot], tile_sem.at[0, 0])
    mask_local = pltpu.make_async_copy(mask_ref.at[zl], mrecv.at[me], mask_sem.at[0, 0])
    for offset in range(1, ring):
        tile_copy(offset).start()
    tile_local.start()
    for offset in range(1, peers):
        mask_copy(offset).start()
    mask_local.start()
    for group in range(groups):
        for offset in range(1, peers):
            in_copy(group, offset).start()
        in_local(group).start()

    gb[...] = jnp.zeros_like(gb)

    tile_local.wait()
    for offset in range(1, ring):
        tile_copy(offset).wait()
    for h in range(2):
        for z in range(zhs):
            pieces = [trecv[z * peers + c, h].astype(F32)[:, :width] for c in range(peers)]
            biasb[h, z, place["x"], place["y"]] = jnp.concatenate(pieces, axis=1).astype(BF16)
    for phase in range(2):
        for h in range(2):
            for way in range(2):
                gather_copy(h, phase, 0, way).start()
        for h in range(2):
            for way in range(2):
                gather_copy(h, phase, 0, way).wait_recv()
                gather_copy(h, phase, 1, way).start()
        if phase == 0:
            mask_local.wait()
            for offset in range(1, peers):
                mask_copy(offset).wait()
            for s in range(peers):
                maskt[s * width : (s + 1) * width, :] = jnp.transpose(mrecv[s])[:width]
            for i in range(rows):
                maskf[i] = jnp.broadcast_to(maskt[:, i : i + 1], (n, LANES))
        for h in range(2):
            for way in range(2):
                gather_copy(h, phase, 0, way).wait_send()
                gather_copy(h, phase, 1, way).wait()

    def widen(r, carry):
        for h in range(2):
            biasf[h, pl.ds(pl.multiple_of(r * tile, tile), tile), :] = biasb[
                h, r // 16, lax.rem(r // 4, 4), lax.rem(r, 4)
            ].astype(F32)
        return carry

    lax.fori_loop(0, n // tile, widen, 0)

    lane_head = lax.broadcasted_iota(jnp.int32, (1, LANES), 1) // HEAD_DIM

    def terms(h, a, zsel):
        axis = orders[h][0]
        return gb[h, zsel, a] if axis == "x" else gb[h, zsel, :, a]

    def first_copy(h, way):
        axis = orders[h][0]
        return remote(
            first_s.at[h, way], first_r.at[h, way], sum_sem.at[h, 0, way], {axis: step(axis, (1, 3)[way])}
        )

    def second_copy(h, way, z):
        axis = orders[h][0]
        return remote(
            second_s.at[h, way, z],
            second_r.at[h, way, z],
            sum_sem.at[h, 1 + z, way],
            {axis: step(axis, (1, 3)[way])},
        )

    def third_copy(h, way):
        axis = orders[h][1]
        return remote(
            third_s.at[h, way], third_r.at[h, way], sum_sem.at[h, 3, way], {axis: step(axis, (1, 3)[way])}
        )

    def fourth_copy(h, way, z):
        axis = orders[h][1]
        return remote(
            fourth_s.at[h, way, z],
            fourth_r.at[h, way, z],
            sum_sem.at[h, 4 + z, way],
            {axis: step(axis, (1, 3)[way])},
        )

    def sums_begin(h):
        axis = orders[h][0]
        for way in range(2):
            first_s[h, way] = terms(h, step(axis, 2), way).astype(BF16)
            first_copy(h, way).start()
        for way in range(2):
            second_s[h, way, 1 - way] = terms(h, step(axis, (1, 3)[way]), 1 - way).astype(BF16)
            second_copy(h, way, 1 - way).start()

    def sums_forward(h):
        axis = orders[h][0]
        for way in range(2):
            first_copy(h, way).wait()
            own = terms(h, step(axis, (1, 3)[way]), way)
            second_s[h, way, way] = (own + first_r[h, way].astype(F32)).astype(BF16)
            second_copy(h, way, way).start()

    def sums_turn(h):
        mine = place[orders[h][0]]
        axis = orders[h][1]
        for z in range(2):
            for way in range(2):
                second_copy(h, way, z).wait()
            partial[h, z] = terms(h, mine, z) + second_r[h, 0, z].astype(F32) + second_r[h, 1, z].astype(F32)
        for way in range(2):
            third_s[h, way] = partial[h, way, step(axis, 2)].astype(BF16)
            third_copy(h, way).start()
        for way in range(2):
            fourth_s[h, way, 1 - way] = partial[h, 1 - way, step(axis, (1, 3)[way])].astype(BF16)
            fourth_copy(h, way, 1 - way).start()

    def sums_close(h):
        axis = orders[h][1]
        for way in range(2):
            third_copy(h, way).wait()
            own = partial[h, way, step(axis, (1, 3)[way])]
            fourth_s[h, way, way] = (own + third_r[h, way].astype(F32)).astype(BF16)
            fourth_copy(h, way, way).start()

    def sums_last(h):
        mine = place[orders[h][1]]
        for z in range(2):
            for way in range(2):
                fourth_copy(h, way, z).wait()
            total = partial[h, z, mine] + fourth_r[h, 0, z].astype(F32) + fourth_r[h, 1, z].astype(F32)
            for c in range(peers):
                piece = total[:, c * width : (c + 1) * width]
                pad = jnp.zeros((tile, LANES - width), F32)
                last_s[z * peers + c, h] = jnp.concatenate([piece, pad], axis=1).astype(BF16)

    def last_copy(offset):
        return remote(
            last_s.at[lax.rem(spot + offset, ring)], last_r.at[spot], last_sem.at[offset], ring_target(offset)
        )

    def one_group(group, carry):
        in_local(group).wait()
        for offset in range(1, peers):
            in_copy(group, offset).wait()

        def prepare(r, carry):
            i = group * 2 + r
            a = ab[i, 0].astype(F32)
            b = ab[i, 1].astype(F32)
            ar = pltpu.roll(a, 64, 1)
            br = pltpu.roll(b, 64, 1)
            for h in range(2):
                kq[r, h] = jnp.where(lane_head == h, ar, 0.0).astype(BF16)
                kq[r, 2 + h] = jnp.where(lane_head == 2 + h, ar, 0.0).astype(BF16)
                vg[r, h] = jnp.where(lane_head == h, br, 0.0).astype(BF16)
                vg[r, 2 + h] = jnp.where(lane_head == h, b, 0.0).astype(BF16)
            kt[r] = jnp.transpose(ar).astype(BF16)
            vk[r] = jnp.zeros_like(vk[r])
            return carry

        lax.fori_loop(0, 2, prepare, 0)

        def one_head(h, carry):
            def one_chunk(t, carry):
                r, ch = t // chunks, lax.rem(t, chunks)
                i = group * 2 + r
                cols = pl.ds(pl.multiple_of(ch * chunk, chunk), chunk)
                s = dot(kq[r, h], ab[i, 0, cols, :], ((1,), (1,)))
                dp = dot(vg[r, h], ab[i, 1, cols, :], ((1,), (1,)))
                m128 = maskf[i]
                mask = jnp.concatenate([m128] * (chunk // LANES), axis=1) if chunk > LANES else m128[:, :chunk]
                s = (s * SCALE + biasf[h, :, cols]) + mask
                top = jnp.max(s, axis=0, keepdims=True)
                e = jnp.exp(s - top)
                inverse = 1.0 / jnp.sum(e, axis=0, keepdims=True)
                delta = jnp.sum(e * dp, axis=0, keepdims=True) * inverse
                p = e * inverse
                ds = p * (dp - delta)
                low = ds.astype(BF16)
                gb[h, :, :, :, :, cols] += ds.reshape(2, 4, 4, tile, chunk)
                vk[r] += dot(p.astype(BF16), vg[r, 2 + h, cols, :], ((1,), (0,))) + dot(
                    low, kq[r, 2 + h, cols, :], ((1,), (0,))
                )
                head_rows = kt[r, pl.ds(pl.multiple_of(h * HEAD_DIM, HEAD_DIM), HEAD_DIM), :]
                at = pl.multiple_of(r * 64 + h * HEAD_DIM, HEAD_DIM)
                dqt[pl.ds(at, HEAD_DIM), cols] = dot(head_rows, low, ((1,), (0,)))
                return carry

            lax.fori_loop(0, 2 * chunks, one_chunk, 0)

            @pl.when((group == groups - 1) & (h == 0))
            def _():
                sums_begin(0)

            return carry

        lax.fori_loop(0, 2, one_head, 0)

        def finish(r, carry):
            obuf[group, r] = (vk[r] * jnp.where(lane_head < 2, 1.0, SCALE)).astype(BF16)
            return carry

        lax.fori_loop(0, 2, finish, 0)
        obuf[group, 2] = (jnp.transpose(dqt[...]) * SCALE).astype(BF16)
        for offset in range(1, peers):
            out_copy(group, offset).start()
        out_local(group).start()
        return carry

    lax.fori_loop(0, groups, one_group, 0)

    sums_begin(1)
    for stage in (sums_forward, sums_turn, sums_close, sums_last):
        for h in range(2):
            stage(h)
    for offset in range(1, ring):
        last_copy(offset).start()
    last_r[spot] = last_s[spot]

    def drain(group, carry):
        out_local(group).wait()
        for offset in range(1, peers):
            out_copy(group, offset).wait()
        return carry

    lax.fori_loop(0, groups, drain, 0)
    for offset in range(1, ring):
        last_copy(offset).wait()
    for c in range(cs):
        for h in range(2):
            total = last_r[c, h].astype(F32)
            for s in range(c + cs, ring, cs):
                total += last_r[s, h].astype(F32)
            gout_ref[2 * c + h] = total


def attention(dims, send, mask, tiles):
    zhs, zls, cs = dims
    width = send.shape[3]
    n = zls * cs * width
    rows = send.shape[1] // zls
    groups = rows // 2
    peers = zls * cs
    ring = zhs * peers
    tile = tiles.shape[2]
    any_spec = pl.BlockSpec(memory_space=pl.ANY)
    vmem_spec = pl.BlockSpec(memory_space=pltpu.VMEM)
    dma = pltpu.SemaphoreType.DMA
    return pl.pallas_call(
        functools.partial(kernel, dims),
        out_shape=(
            jax.ShapeDtypeStruct((cs, zls * groups, 3, width, LANES), BF16),
            jax.ShapeDtypeStruct((HEADS, tile, LANES), F32),
        ),
        in_specs=[any_spec, any_spec, any_spec],
        out_specs=(any_spec, vmem_spec),
        scratch_shapes=[
            pltpu.VMEM((rows, 2, n, LANES), BF16),
            pltpu.VMEM((2, 2, 4, 4, tile, n), BF16),
            pltpu.VMEM((2, n, n), F32),
            pltpu.VMEM((2, 2, 4, 4, tile, n), F32),
            pltpu.VMEM((peers, 8, LANES), F32),
            pltpu.VMEM((n, 8), F32),
            pltpu.VMEM((rows, n, LANES), F32),
            pltpu.VMEM((2, 4, n, LANES), BF16),
            pltpu.VMEM((2, 4, n, LANES), BF16),
            pltpu.VMEM((2, LANES, n), BF16),
            pltpu.VMEM((2, n, LANES), F32),
            pltpu.VMEM((LANES, n), F32),
            pltpu.VMEM((groups, 3, n, LANES), BF16),
            pltpu.VMEM((ring, 2, tile, LANES), BF16),
            pltpu.VMEM((2, 2, 4, tile, n), BF16),
            pltpu.VMEM((2, 2, 4, tile, n), BF16),
            pltpu.VMEM((2, 2, 2, 4, tile, n), BF16),
            pltpu.VMEM((2, 2, 2, 4, tile, n), BF16),
            pltpu.VMEM((2, 2, 4, tile, n), F32),
            pltpu.VMEM((2, 2, tile, n), BF16),
            pltpu.VMEM((2, 2, tile, n), BF16),
            pltpu.VMEM((2, 2, 2, tile, n), BF16),
            pltpu.VMEM((2, 2, 2, tile, n), BF16),
            pltpu.VMEM((ring, 2, tile, LANES), BF16),
            pltpu.VMEM((ring, 2, tile, LANES), BF16),
            dma((peers, 2)),
            dma((groups, peers, 2)),
            dma((groups,)),
            dma((groups, peers, 2)),
            dma((groups,)),
            dma((ring, 2)),
            dma((2, 2, 2, 2, 2)),
            dma((2, 6, 2, 2)),
            dma((ring, 2)),
        ],
        compiler_params=pltpu.CompilerParams(
            collective_id=0, has_side_effects=True, vmem_limit_bytes=60 * 1024 * 1024
        ),
        cost_estimate=pl.CostEstimate(
            flops=10 * rows * 2 * n * n * LANES, bytes_accessed=32 * 1024 * 1024, transcendentals=0
        ),
        name="attention_backward",
    )(send, mask, tiles)


def local(zhs, zs, cs, query_proj, key_proj, value_proj, pair_bias, pair_mask, grad_out):
    rows, width, _ = query_proj.shape
    half = HEADS // 2 * HEAD_DIM
    tile = pair_bias.shape[2]
    tiles = jnp.transpose(pair_bias, (0, 2, 1)).reshape(cs, 2, tile, width)
    tiles = jnp.pad(tiles, ((0, 0), (0, 0), (0, 0), (0, LANES - width)))

    def pack(a, b):
        return jnp.stack(
            [jnp.concatenate([a[..., c * half : (c + 1) * half], b[..., c * half : (c + 1) * half]], -1) for c in range(cs)]
        )

    send = jnp.stack([pack(query_proj, key_proj), pack(grad_out, value_proj)], 2)
    mask = 1000000000.0 * (pair_mask.astype(F32) - 1.0)
    per_chip = rows // zs
    mask = jnp.pad(mask.reshape(zs, per_chip, width), ((0, 0), (0, 8 - per_chip), (0, LANES - width)))

    out, gb = attention((zhs, zs, cs), send, mask, tiles)
    grad_bias = jnp.transpose(gb[:, :, :width], (0, 2, 1))

    def rejoin(pieces):
        return jnp.concatenate([pieces[c] for c in range(cs)], axis=-1)

    value_key = out[:, :, :2].reshape(cs, rows, width, LANES)
    grad_value = rejoin(value_key[..., :half])
    grad_key = rejoin(value_key[..., half:])
    pairs = out[:, :, 2]
    pairs = jnp.stack([pairs[..., :half], pairs[..., half:]], axis=2).reshape(cs, rows, width, half)
    grad_query = rejoin(pairs)
    return grad_query, grad_key, grad_value, grad_bias


def solution(mesh):
    shape = (2, 4, 4, mesh.shape["col"] // 2, 2)
    torus = Mesh(mesh.devices.reshape(shape), ROW + COL)
    pair = P(ROW, COL, None)
    tile = P(None, COL, ROW)
    return jax.shard_map(
        functools.partial(local, shape[0], shape[3], shape[4]),
        mesh=torus,
        in_specs=(pair, pair, pair, tile, P(ROW, COL), pair),
        out_specs=(pair, pair, pair, tile),
        check_vma=False,
    )
```

time: 504 us -> 136 us (0.27)
  waiting for transfers between devices: 341 us -> 0 us
  blocking collectives: 18.4 us -> 0 us
  Pallas kernels: 101 us -> 119 us
  between operations: 14.2 us -> 0.81 us
  starting transfers between devices: 7.02 us -> 0 us
    reduce_scatter x1 -> x0, waiting for transfers between devices: 257 us -> none  [local(): gb = lax.psum_scatter(gb, ROW, scatter_dimension=0, tiled=False)]
    all_gather x1 -> x0, waiting for transfers between devices: 81.5 us -> none  [local(): bias = lax.all_gather(bias, ROW, axis=0, tiled=False)]
    all_gather x1 -> x0, blocking collectives: 18.4 us -> none  [local(): bias = lax.all_gather(bias, COL, axis=2, tiled=True)]
    pallas_call x1, Pallas kernels: 101 us -> 119 us  [attention(): pl.pallas_call(functools.partial(kernel, dims), out_shape=(jax.ShapeDtype...]
    all_to_all x1 -> x0, starting transfers between devices: 6.94 us -> none  [local(): gb = lax.all_to_all(gb, COL, split_axis=0, concat_axis=0, tiled=True)]
  transfers between devices with their start and end apart: 3 -> 0, of which waited for: 3 -> 0; matrix products, arithmetic and copies ran while one was open for 2% -> 0% of each run, Pallas kernels for 0% -> 0%
where the time goes in v2:
time: 136 us
  Pallas kernels  119 us (88%)
  local copies, waits for them, and re-layouts  9.7 us (7%)
  other arithmetic  5.93 us (4%)
    pallas_call x1, Pallas kernels, attention(): pl.pallas_call(functools.partial(kernel, dims), out_shape=(jax.ShapeDtype...  119 us
    unnamed x15, local copies, waits for them, and re-layouts  3.09 us

profile of v2, /device:TPU:1, one launch (start us, length us, event | category | flops | bytes accessed | tf_op | source)
XLA Modules:
  0.0 135.8 jit_solution(4041077975580358950)
XLA Ops:
  0.6 0.0 copy-start
  0.6 1.6 %fusion.1 = (bf16[24,96,64]{2,1,0:T(8,128)(2,1)S(1)}, bf16[24,96,64]{2,1,0:T(8,128)(2,1)S(1)}) fusion(bf16[24,96,128]{2,1,0:T(8,128)(2,1)} %param.6), kind=kLoop, calls=%fused_computation.23 | loop fusion | bytes 1179648 | tf_op jit(solution)/shard_map/slice | solution.py:492
  2.3 0.0 copy-done
  2.3 0.2 fusion.2
  2.5 0.7 maximum_bitcast_fusion.2
  3.2 0.0 copy-start.1
  3.2 0.1 maximum_bitcast_fusion
  3.3 0.9 copy-done.1
  4.2 0.0 copy-start.2
  4.2 0.2 fusion.3
  4.5 0.8 copy-done.2
  5.3 0.2 fusion.4
  5.5 0.7 maximum_bitcast_fusion.4
  6.2 0.1 maximum_bitcast_fusion.1
  6.3 0.0 copy-start.6
  6.3 0.0 copy-start.5
  6.3 1.7 %pad_maximum_fusion.send_ref = bf16[2,24,2,96,128]{4,3,2,1,0:T(8,128)(2,1)} fusion(bf16[2,24,1,96,128]{4,3,2,1,0:T(8,128)(2,1)S(1)} %maximum_bitcast_fusion.1, bf16[2,24,1,96,128]{4,3,2,1,0:T(8,128)(2,1)S(1)} %maximum_bitcast_fusion), kind=kLoop, calls=%fused_computation | loop fusion | flops 1179648 | bytes 4718592 | tf_op jit(solution)/shard_map/stack | solution.py:495
  8.0 0.0 copy-done.6
  8.0 0.6 pad.8.mask_ref
  8.6 0.0 copy-done.5
  8.6 0.6 pad.9.tile_ref
  9.3 119.4 %attention_backward.1 = (bf16[2,12,3,96,128]{4,3,2,1,0:T(8,128)(2,1)}, f32[4,24,128]{2,1,0:T(8,128)}) custom-call(bf16[2,24,2,96,128]{4,3,2,1,0:T(8,128)(2,1)} %pad_maximum_fusion.send_ref, f32[4,8,128]{2,1,0:T(8,128)} %pad.8.mask_ref, bf16[2,2,24,128]{3,2,1,0:T(8,128)(2,1)} %pad.9.tile_ref), custom_call_target="tpu_custom_call" | custom-call | flops 9059696640 | bytes 33554432 | tf_op jit(solution)/shard_map/attention_backward/pallas_call | solution.py:429
  128.7 1.1 slice_bitcast_fusion.6
  129.8 0.2 slice_bitcast_fusion.5
  130.0 0.2 fusion
  130.3 0.3 copy.10
  130.5 0.3 copy.11
  130.8 0.0 copy-start.3
  130.8 0.2 pad_maximum_fusion.1
  131.0 1.1 copy.12
  132.1 0.2 copy-done.3
  132.3 0.1 slice.78
  132.5 0.4 slice_bitcast_fusion.1
  132.9 1.1 pad_maximum_fusion.4
  134.1 0.0 copy-start.4
  134.1 1.1 pad_maximum_fusion.3
  135.2 0.0 copy-done.4
  135.2 0.6 slice_bitcast_fusion.7
  (2 shorter events, 0.0 us)
Async XLA Ops:
  0.6 1.6 %copy-start = (bf16[24,96,128]{2,1,0:T(8,128)(2,1)S(1)}, bf16[24,96,128]{2,1,0:T(8,128)(2,1)}, u32[]{:S(2)}) copy-start(bf16[24,96,128]{2,1,0:T(8,128)(2,1)} %param.7) | copy-start | bytes 1769476
  3.2 1.1 copy-start.1
  4.2 1.1 copy-start.2
  6.3 1.7 %copy-start.6 = (s32[24,96]{1,0:T(8,128)S(1)}, s32[24,96]{1,0:T(8,128)}, u32[]{:S(2)}) copy-start(s32[24,96]{1,0:T(8,128)} %param.10) | copy-start | bytes 27652
  6.3 2.3 %copy-start.5 = (bf16[4,96,24]{1,2,0:T(8,128)(2,1)S(1)}, bf16[4,96,24]{1,2,0:T(8,128)(2,1)}, u32[]{:S(2)}) copy-start(bf16[4,96,24]{1,2,0:T(8,128)(2,1)} %param.9) | copy-start | bytes 55300
  130.8 1.5 %copy-start.3 = (bf16[2,12,3,96,128]{4,3,2,1,0:T(8,128)(2,1)S(1)}, bf16[2,12,3,96,128]{4,3,2,1,0:T(8,128)(2,1)}, u32[]{:S(2)}) copy-start(bf16[2,12,3,96,128]{4,3,2,1,0:T(8,128)(2,1)} %get-tuple-element.6) | copy-start | bytes 5308420
  134.1 1.1 copy-start.4

commit v3 on v2

--- a/solution.py
+++ b/solution.py
@@ -27,11 +27,23 @@
 
 def kernel(
     dims,
-    send_ref,
+    q_ref,
+    k_ref,
+    v_ref,
+    g_ref,
     mask_ref,
     tile_ref,
+    dq_ref,
+    dk_ref,
+    dv_ref,
+    gout_ref,
+    send_ref,
     out_ref,
-    gout_ref,
+    pbuf,
+    sbuf,
+    dpbuf,
+    lowbuf,
+    maxbuf,
     ab,
     biasb,
     biasf,
@@ -59,9 +71,7 @@
     last_r,
     mask_sem,
     in_sem,
-    in_lsem,
     out_sem,
-    out_lsem,
     tile_sem,
     gather_sem,
     sum_sem,
@@ -69,7 +79,7 @@
 ):
     zhs, zls, cs = dims
     n = ab.shape[2]
-    width = send_ref.shape[3]
+    width = q_ref.shape[1]
     tile = tile_ref.shape[2]
     rows = ab.shape[0]
     groups = rows // 2
@@ -77,6 +87,7 @@
     ring = zhs * peers
     chunk = min(CHUNK, n)
     chunks = n // chunk
+    span = n // 8
     zh, zl, core = lax.axis_index("zh"), lax.axis_index("zl"), lax.axis_index("core")
     place = {"x": lax.axis_index("x"), "y": lax.axis_index("y")}
     me = zl * cs + core
@@ -107,6 +118,40 @@
     def step(axis, by):
         return lax.rem(place[axis] + by, 4)
 
+    low_half = lax.broadcasted_iota(jnp.int32, (1, 1, LANES), 2) < LANES // 2
+
+    def join(a, b):
+        a, b = a.astype(F32), b.astype(F32)
+        shape = a.shape
+        turn = lambda v: pltpu.roll(v.reshape(-1, LANES), LANES // 2, 1).reshape(shape)
+        return jnp.where(low_half, a, turn(b)).astype(BF16), jnp.where(low_half, turn(a), b).astype(BF16)
+
+    def pack(group):
+        def pack_chip(z, carry):
+            at = pl.ds(z * rows + group * 2, 2)
+            first = join(q_ref[at], k_ref[at])
+            second = join(g_ref[at], v_ref[at])
+            for c in range(2):
+                send_ref[c, at, 0] = first[c]
+                send_ref[c, at, 1] = second[c]
+            return carry
+
+        lax.fori_loop(0, zls, pack_chip, 0)
+
+    def unpack(group):
+        def unpack_chip(z, carry):
+            at = z * rows + group * 2
+            pair = z * groups + group
+            value, key = join(out_ref[0, pair, :2], out_ref[1, pair, :2])
+            dv_ref[pl.ds(at, 2)] = value
+            dk_ref[pl.ds(at, 2)] = key
+            even, odd = join(out_ref[0, pair, 2:], out_ref[1, pair, 2:])
+            dq_ref[pl.ds(at, 1)] = even
+            dq_ref[pl.ds(at + 1, 1)] = odd
+            return carry
+
+        lax.fori_loop(0, zls, unpack_chip, 0)
+
     barrier = pltpu.get_barrier_semaphore()
     for offset in range(1, ring):
         pl.semaphore_signal(barrier, inc=1, device_id=ring_target(offset), device_id_type=MESH)
@@ -135,13 +180,6 @@
             {"zl": z, "core": c},
         )
 
-    def in_local(group):
-        return pltpu.make_async_copy(
-            send_ref.at[core, pl.ds(zl * rows + group * 2, 2)],
-            ab.at[pl.ds(group * 2, 2), :, columns_of(me)],
-            in_lsem.at[group],
-        )
-
     def out_copy(group, offset):
         other, z, c = peer_of(offset)
         return remote(
@@ -149,13 +187,6 @@
             out_ref.at[core, zl * groups + group],
             out_sem.at[group, offset],
             {"zl": z, "core": c},
-        )
-
-    def out_local(group):
-        return pltpu.make_async_copy(
-            obuf.at[group, :, columns_of(me)],
-            out_ref.at[core, zl * groups + group],
-            out_lsem.at[group],
         )
 
     orders = (("x", "y"), ("y", "x"))
@@ -175,27 +206,25 @@
             ref = block(h, phase, step(axis, 4 - by), way)
         return remote(ref, ref, gather_sem.at[h, phase, hop, way], {axis: step(axis, by)})
 
-    tile_local = pltpu.make_async_copy(tile_ref.at[core], trecv.at[spot], tile_sem.at[0, 0])
-    mask_local = pltpu.make_async_copy(mask_ref.at[zl], mrecv.at[me], mask_sem.at[0, 0])
     for offset in range(1, ring):
         tile_copy(offset).start()
-    tile_local.start()
+    trecv[spot] = tile_ref[core]
     for offset in range(1, peers):
         mask_copy(offset).start()
-    mask_local.start()
+    mrecv[me] = mask_ref[zl]
     for group in range(groups):
+        pack(group)
         for offset in range(1, peers):
             in_copy(group, offset).start()
-        in_local(group).start()
+        ab[group * 2 : group * 2 + 2, :, columns_of(me)] = send_ref[core, pl.ds(zl * rows + group * 2, 2)]
 
     gb[...] = jnp.zeros_like(gb)
 
-    tile_local.wait()
     for offset in range(1, ring):
         tile_copy(offset).wait()
     for h in range(2):
         for z in range(zhs):
-            pieces = [trecv[z * peers + c, h].astype(F32)[:, :width] for c in range(peers)]
+            pieces = [trecv[z * peers + c, h].astype(F32) for c in range(peers)]
             biasb[h, z, place["x"], place["y"]] = jnp.concatenate(pieces, axis=1).astype(BF16)
     for phase in range(2):
         for h in range(2):
@@ -206,11 +235,10 @@
                 gather_copy(h, phase, 0, way).wait_recv()
                 gather_copy(h, phase, 1, way).start()
         if phase == 0:
-            mask_local.wait()
             for offset in range(1, peers):
                 mask_copy(offset).wait()
             for s in range(peers):
-                maskt[s * width : (s + 1) * width, :] = jnp.transpose(mrecv[s])[:width]
+                maskt[s * width : (s + 1) * width, :] = jnp.transpose(mrecv[s])
             for i in range(rows):
                 maskf[i] = jnp.broadcast_to(maskt[:, i : i + 1], (n, LANES))
         for h in range(2):
@@ -309,9 +337,7 @@
                 fourth_copy(h, way, z).wait()
             total = partial[h, z, mine] + fourth_r[h, 0, z].astype(F32) + fourth_r[h, 1, z].astype(F32)
             for c in range(peers):
-                piece = total[:, c * width : (c + 1) * width]
-                pad = jnp.zeros((tile, LANES - width), F32)
-                last_s[z * peers + c, h] = jnp.concatenate([piece, pad], axis=1).astype(BF16)
+                last_s[z * peers + c, h] = total[:, c * width : (c + 1) * width].astype(BF16)
 
     def last_copy(offset):
         return remote(
@@ -319,7 +345,6 @@
         )
 
     def one_group(group, carry):
-        in_local(group).wait()
         for offset in range(1, peers):
             in_copy(group, offset).wait()
 
@@ -340,41 +365,76 @@
 
         lax.fori_loop(0, 2, prepare, 0)
 
-        def one_head(h, carry):
-            def one_chunk(t, carry):
-                r, ch = t // chunks, lax.rem(t, chunks)
-                i = group * 2 + r
-                cols = pl.ds(pl.multiple_of(ch * chunk, chunk), chunk)
-                s = dot(kq[r, h], ab[i, 0, cols, :], ((1,), (1,)))
-                dp = dot(vg[r, h], ab[i, 1, cols, :], ((1,), (1,)))
-                m128 = maskf[i]
+        def where_of(u):
+            h, ch = u // chunks, lax.rem(u, chunks)
+            return h, pl.ds(pl.multiple_of(ch * chunk, chunk), chunk)
+
+        def scores(r, u):
+            h, cols = where_of(u)
+            i = group * 2 + r
+            s = dot(kq[r, h], ab[i, 0, cols, :], ((1,), (1,)))
+            top = None
+            for k0 in range(0, n, span):
+                m128 = maskf[i, k0 : k0 + span, :]
                 mask = jnp.concatenate([m128] * (chunk // LANES), axis=1) if chunk > LANES else m128[:, :chunk]
-                s = (s * SCALE + biasf[h, :, cols]) + mask
-                top = jnp.max(s, axis=0, keepdims=True)
-                e = jnp.exp(s - top)
-                inverse = 1.0 / jnp.sum(e, axis=0, keepdims=True)
-                delta = jnp.sum(e * dp, axis=0, keepdims=True) * inverse
-                p = e * inverse
-                ds = p * (dp - delta)
-                low = ds.astype(BF16)
-                gb[h, :, :, :, :, cols] += ds.reshape(2, 4, 4, tile, chunk)
-                vk[r] += dot(p.astype(BF16), vg[r, 2 + h, cols, :], ((1,), (0,))) + dot(
-                    low, kq[r, 2 + h, cols, :], ((1,), (0,))
-                )
-                head_rows = kt[r, pl.ds(pl.multiple_of(h * HEAD_DIM, HEAD_DIM), HEAD_DIM), :]
-                at = pl.multiple_of(r * 64 + h * HEAD_DIM, HEAD_DIM)
-                dqt[pl.ds(at, HEAD_DIM), cols] = dot(head_rows, low, ((1,), (0,)))
-                return carry
-
-            lax.fori_loop(0, 2 * chunks, one_chunk, 0)
-
-            @pl.when((group == groups - 1) & (h == 0))
+                part = (s[k0 : k0 + span] * SCALE + biasf[h, k0 : k0 + span, cols]) + mask
+                sbuf[r, k0 : k0 + span] = part
+                part = jnp.max(part.reshape(-1, 8, chunk), axis=0)
+                top = part if top is None else jnp.maximum(top, part)
+            maxbuf[r] = top
+            dpbuf[r] = dot(vg[r, h], ab[i, 1, cols, :], ((1,), (1,)))
+
+        def soft(r, u):
+            h, cols = where_of(u)
+            top = jnp.max(maxbuf[r], axis=0, keepdims=True)
+            total = weighted = None
+            for k0 in range(0, n, span):
+                e = jnp.exp(sbuf[r, k0 : k0 + span] - top)
+                sbuf[r, k0 : k0 + span] = e
+                first = jnp.sum(e.reshape(-1, 8, chunk), axis=0)
+                second = jnp.sum((e * dpbuf[r, k0 : k0 + span]).reshape(-1, 8, chunk), axis=0)
+                total = first if total is None else total + first
+                weighted = second if weighted is None else weighted + second
+            inverse = 1.0 / jnp.sum(total, axis=0, keepdims=True)
+            delta = jnp.sum(weighted, axis=0, keepdims=True) * inverse
+            for b in range(8):
+                k0 = b * span
+                p = sbuf[r, k0 : k0 + span] * inverse
+                ds = p * (dpbuf[r, k0 : k0 + span] - delta)
+                pbuf[r, k0 : k0 + span] = p.astype(BF16)
+                lowbuf[r, k0 : k0 + span] = ds.astype(BF16)
+                gb[h, b // 4, b % 4, :, :, cols] += ds.reshape(4, tile, chunk)
+
+        def grads(r, u):
+            h, cols = where_of(u)
+            vk[r] += dot(pbuf[r], vg[r, 2 + h, cols, :], ((1,), (0,))) + dot(
+                lowbuf[r], kq[r, 2 + h, cols, :], ((1,), (0,))
+            )
+            head_rows = kt[r, pl.ds(pl.multiple_of(h * HEAD_DIM, HEAD_DIM), HEAD_DIM), :]
+            at = pl.multiple_of(r * 64 + h * HEAD_DIM, HEAD_DIM)
+            dqt[pl.ds(at, HEAD_DIM), cols] = dot(head_rows, lowbuf[r], ((1,), (0,)))
+
+        steps = 2 * chunks
+        pbuf[1] = jnp.zeros_like(pbuf[1])
+        lowbuf[1] = jnp.zeros_like(lowbuf[1])
+        scores(0, 0)
+
+        def one_step(u, carry):
+            scores(1, u)
+            grads(1, lax.rem(u + steps - 1, steps))
+            soft(0, u)
+            scores(0, lax.rem(u + 1, steps))
+            grads(0, u)
+            soft(1, u)
+
+            @pl.when((group == groups - 1) & (u == chunks - 1))
             def _():
                 sums_begin(0)
 
             return carry
 
-        lax.fori_loop(0, 2, one_head, 0)
+        lax.fori_loop(0, steps, one_step, 0)
+        grads(1, steps - 1)
 
         def finish(r, carry):
             obuf[group, r] = (vk[r] * jnp.where(lane_head < 2, 1.0, SCALE)).astype(BF16)
@@ -384,7 +444,7 @@
         obuf[group, 2] = (jnp.transpose(dqt[...]) * SCALE).astype(BF16)
         for offset in range(1, peers):
             out_copy(group, offset).start()
-        out_local(group).start()
+        out_ref[core, zl * groups + group] = obuf[group, :, columns_of(me)]
         return carry
 
     lax.fori_loop(0, groups, one_group, 0)
@@ -398,9 +458,9 @@
     last_r[spot] = last_s[spot]
 
     def drain(group, carry):
-        out_local(group).wait()
         for offset in range(1, peers):
             out_copy(group, offset).wait()
+        unpack(group)
         return carry
 
     lax.fori_loop(0, groups, drain, 0)
@@ -414,33 +474,42 @@
             gout_ref[2 * c + h] = total
 
 
-def attention(dims, send, mask, tiles):
+def attention(dims, queries, keys, values, grads, mask, tiles):
     zhs, zls, cs = dims
-    width = send.shape[3]
+    width = queries.shape[1]
     n = zls * cs * width
-    rows = send.shape[1] // zls
+    rows = queries.shape[0] // zls
+    chunk = min(CHUNK, n)
     groups = rows // 2
     peers = zls * cs
     ring = zhs * peers
     tile = tiles.shape[2]
-    any_spec = pl.BlockSpec(memory_space=pl.ANY)
     vmem_spec = pl.BlockSpec(memory_space=pltpu.VMEM)
     dma = pltpu.SemaphoreType.DMA
     return pl.pallas_call(
         functools.partial(kernel, dims),
         out_shape=(
-            jax.ShapeDtypeStruct((cs, zls * groups, 3, width, LANES), BF16),
-            jax.ShapeDtypeStruct((HEADS, tile, LANES), F32),
+            jax.ShapeDtypeStruct(queries.shape, BF16),
+            jax.ShapeDtypeStruct(queries.shape, BF16),
+            jax.ShapeDtypeStruct(queries.shape, BF16),
+            jax.ShapeDtypeStruct((HEADS, tile, width), F32),
         ),
-        in_specs=[any_spec, any_spec, any_spec],
-        out_specs=(any_spec, vmem_spec),
+        in_specs=[vmem_spec] * 6,
+        out_specs=(vmem_spec,) * 4,
         scratch_shapes=[
+            pltpu.VMEM((cs, zls * rows, 2, width, LANES), BF16),
+            pltpu.VMEM((cs, zls * groups, 3, width, LANES), BF16),
+            pltpu.VMEM((2, n, chunk), BF16),
+            pltpu.VMEM((2, n, chunk), F32),
+            pltpu.VMEM((2, n, chunk), F32),
+            pltpu.VMEM((2, n, chunk), BF16),
+            pltpu.VMEM((2, 8, chunk), F32),
             pltpu.VMEM((rows, 2, n, LANES), BF16),
             pltpu.VMEM((2, 2, 4, 4, tile, n), BF16),
             pltpu.VMEM((2, n, n), F32),
             pltpu.VMEM((2, 2, 4, 4, tile, n), F32),
-            pltpu.VMEM((peers, 8, LANES), F32),
-            pltpu.VMEM((n, 8), F32),
+            pltpu.VMEM((peers, rows, width), F32),
+            pltpu.VMEM((n, rows), F32),
             pltpu.VMEM((rows, n, LANES), F32),
             pltpu.VMEM((2, 4, n, LANES), BF16),
             pltpu.VMEM((2, 4, n, LANES), BF16),
@@ -448,7 +517,7 @@
             pltpu.VMEM((2, n, LANES), F32),
             pltpu.VMEM((LANES, n), F32),
             pltpu.VMEM((groups, 3, n, LANES), BF16),
-            pltpu.VMEM((ring, 2, tile, LANES), BF16),
+            pltpu.VMEM((ring, 2, tile, width), BF16),
             pltpu.VMEM((2, 2, 4, tile, n), BF16),
             pltpu.VMEM((2, 2, 4, tile, n), BF16),
             pltpu.VMEM((2, 2, 2, 4, tile, n), BF16),
@@ -458,58 +527,36 @@
             pltpu.VMEM((2, 2, tile, n), BF16),
             pltpu.VMEM((2, 2, 2, tile, n), BF16),
             pltpu.VMEM((2, 2, 2, tile, n), BF16),
-            pltpu.VMEM((ring, 2, tile, LANES), BF16),
-            pltpu.VMEM((ring, 2, tile, LANES), BF16),
+            pltpu.VMEM((ring, 2, tile, width), BF16),
+            pltpu.VMEM((ring, 2, tile, width), BF16),
             dma((peers, 2)),
             dma((groups, peers, 2)),
-            dma((groups,)),
             dma((groups, peers, 2)),
-            dma((groups,)),
             dma((ring, 2)),
             dma((2, 2, 2, 2, 2)),
             dma((2, 6, 2, 2)),
             dma((ring, 2)),
         ],
         compiler_params=pltpu.CompilerParams(
-            collective_id=0, has_side_effects=True, vmem_limit_bytes=60 * 1024 * 1024
+            collective_id=0, has_side_effects=True, vmem_limit_bytes=63 * 1024 * 1024
         ),
         cost_estimate=pl.CostEstimate(
             flops=10 * rows * 2 * n * n * LANES, bytes_accessed=32 * 1024 * 1024, transcendentals=0
         ),
         name="attention_backward",
-    )(send, mask, tiles)
+    )(queries, keys, values, grads, mask, tiles)
 
 
 def local(zhs, zs, cs, query_proj, key_proj, value_proj, pair_bias, pair_mask, grad_out):
     rows, width, _ = query_proj.shape
-    half = HEADS // 2 * HEAD_DIM
     tile = pair_bias.shape[2]
     tiles = jnp.transpose(pair_bias, (0, 2, 1)).reshape(cs, 2, tile, width)
-    tiles = jnp.pad(tiles, ((0, 0), (0, 0), (0, 0), (0, LANES - width)))
-
-    def pack(a, b):
-        return jnp.stack(
-            [jnp.concatenate([a[..., c * half : (c + 1) * half], b[..., c * half : (c + 1) * half]], -1) for c in range(cs)]
-        )
-
-    send = jnp.stack([pack(query_proj, key_proj), pack(grad_out, value_proj)], 2)
     mask = 1000000000.0 * (pair_mask.astype(F32) - 1.0)
-    per_chip = rows // zs
-    mask = jnp.pad(mask.reshape(zs, per_chip, width), ((0, 0), (0, 8 - per_chip), (0, LANES - width)))
-
-    out, gb = attention((zhs, zs, cs), send, mask, tiles)
-    grad_bias = jnp.transpose(gb[:, :, :width], (0, 2, 1))
-
-    def rejoin(pieces):
-        return jnp.concatenate([pieces[c] for c in range(cs)], axis=-1)
-
-    value_key = out[:, :, :2].reshape(cs, rows, width, LANES)
-    grad_value = rejoin(value_key[..., :half])
-    grad_key = rejoin(value_key[..., half:])
-    pairs = out[:, :, 2]
-    pairs = jnp.stack([pairs[..., :half], pairs[..., half:]], axis=2).reshape(cs, rows, width, half)
-    grad_query = rejoin(pairs)
-    return grad_query, grad_key, grad_value, grad_bias
+    mask = mask.reshape(zs, rows // zs, width)
+    grad_query, grad_key, grad_value, gb = attention(
+        (zhs, zs, cs), query_proj, key_proj, value_proj, grad_out, mask, tiles
+    )
+    return grad_query, grad_key, grad_value, jnp.transpose(gb, (0, 2, 1))
 
 
 def solution(mesh):

time: 136 us -> 124 us (0.912)
  other arithmetic: 5.93 us -> 0.71 us
  local copies, waits for them, and re-layouts: 9.7 us -> 5.31 us
  Pallas kernels: 119 us -> 117 us
    another operation x6 -> x0, other arithmetic: 3.44 us -> none  [the longest x3 1.89 us: local(): jnp.stack([pack(query_proj, key_proj), pack(grad_out, value_proj)], 2)]
    slice x7 -> x0, local copies, waits for them, and re-layouts: 2.96 us -> none  [the longest x2 1.84 us: pack(): a[..., c * half:(c + 1) * half]]
    concatenate x3 -> x0, other arithmetic: 2.49 us -> none  [rejoin(): return jnp.concatenate([pieces[c] for c in range(cs)], axis=-1)]
    pallas_call x1, Pallas kernels: 119 us -> 117 us  [attention(): pl.pallas_call(functools.partial(kernel, dims), out_shape=(jax.ShapeDtype...]
    unnamed x15 -> x10, local copies, waits for them, and re-layouts: 3.09 us -> 4.7 us
    squeeze x2 -> x0, local copies, waits for them, and re-layouts: 1.55 us -> none  [the longest x1 1.11 us: local(): pairs = out[:, :, 2]]
where the time goes in v3:
time: 124 us
  Pallas kernels  117 us (94%)
  local copies, waits for them, and re-layouts  5.31 us (4%)
    pallas_call x1, Pallas kernels, attention(): pl.pallas_call(functools.partial(kernel, dims), out_shape=(jax.ShapeDtype...  117 us
    unnamed x10, local copies, waits for them, and re-layouts  4.7 us

profile of v3, /device:TPU:1, one launch (start us, length us, event | category | flops | bytes accessed | tf_op | source)
XLA Modules:
  0.0 124.0 jit_solution(15694738058362673319)
XLA Ops:
  0.6 0.7 add_multiply_fusion
  1.3 0.6 reshape.14.mask_ref
  2.0 117.4 %attention_backward.1 = (bf16[24,96,128]{2,1,0:T(8,128)(2,1)}, bf16[24,96,128]{2,1,0:T(8,128)(2,1)}, bf16[24,96,128]{2,1,0:T(8,128)(2,1)}, f32[4,24,96]{2,1,0:T(8,128)}) custom-call(bf16[24,96,128]{2,1,0:T(8,128)(2,1)} %q_ref.1, bf16[24,96,128]{2,1,0:T(8,128)(2,1)} %k_ref.1, bf16[24,96,128]{2,1,0:T(8,128)(2,1)} %v_ref.1, bf16[24,96,128]{2,1,0:T(8,128)(2,1)} %g_ref.1, ...), custom_call_target="tpu_custom_call" | custom-call | flops 9059696640 | bytes 33554432 | tf_op jit(solution)/shard_map/attention_backward/pallas_call | solution.py:489
  119.3 0.0 copy-start.1
  119.3 2.0 %copy.14 = bf16[24,96,128]{2,1,0:T(8,128)(2,1)} copy(bf16[24,96,128]{2,1,0:T(8,128)(2,1)} %get-tuple-element.16) | data formatting | bytes 1179648
  121.3 0.0 copy-done.1
  121.3 0.0 copy-start
  121.3 0.8 copy.15
  122.1 0.5 copy-done
  122.6 0.0 copy-start.2
  122.6 0.8 copy.16
  123.4 0.0 copy-done.2
  123.4 0.6 copy.17
Async XLA Ops:
  119.3 2.0 %copy-start.1 = (bf16[24,96,128]{2,1,0:T(8,128)(2,1)S(1)}, bf16[24,96,128]{2,1,0:T(8,128)(2,1)}, u32[]{:S(2)}) copy-start(bf16[24,96,128]{2,1,0:T(8,128)(2,1)} %get-tuple-element.17) | copy-start | bytes 1769476
  121.3 1.3 %copy-start = (bf16[24,96,128]{2,1,0:T(8,128)(2,1)S(1)}, bf16[24,96,128]{2,1,0:T(8,128)(2,1)}, u32[]{:S(2)}) copy-start(bf16[24,96,128]{2,1,0:T(8,128)(2,1)} %get-tuple-element.18) | copy-start | bytes 1769476
  122.6 0.8 copy-start.2

commit v4 on v3

--- a/solution.py
+++ b/solution.py
@@ -27,16 +27,17 @@
 
 def kernel(
     dims,
-    q_ref,
-    k_ref,
-    v_ref,
-    g_ref,
+    q_hbm,
+    k_hbm,
+    v_hbm,
+    g_hbm,
     mask_ref,
     tile_ref,
     dq_ref,
     dk_ref,
     dv_ref,
     gout_ref,
+    loaded,
     send_ref,
     out_ref,
     pbuf,
@@ -69,6 +70,7 @@
     fourth_r,
     last_s,
     last_r,
+    load_sem,
     mask_sem,
     in_sem,
     out_sem,
@@ -79,7 +81,7 @@
 ):
     zhs, zls, cs = dims
     n = ab.shape[2]
-    width = q_ref.shape[1]
+    width = loaded.shape[2]
     tile = tile_ref.shape[2]
     rows = ab.shape[0]
     groups = rows // 2
@@ -129,8 +131,8 @@
     def pack(group):
         def pack_chip(z, carry):
             at = pl.ds(z * rows + group * 2, 2)
-            first = join(q_ref[at], k_ref[at])
-            second = join(g_ref[at], v_ref[at])
+            first = join(loaded[0, at], loaded[1, at])
+            second = join(loaded[3, at], loaded[2, at])
             for c in range(2):
                 send_ref[c, at, 0] = first[c]
                 send_ref[c, at, 1] = second[c]
@@ -141,11 +143,11 @@
     def unpack(group):
         def unpack_chip(z, carry):
             at = z * rows + group * 2
-            pair = z * groups + group
-            value, key = join(out_ref[0, pair, :2], out_ref[1, pair, :2])
+            pair = zls * rows + z * groups + group
+            value, key = join(out_ref[0, pl.ds(at, 2)], out_ref[1, pl.ds(at, 2)])
             dv_ref[pl.ds(at, 2)] = value
             dk_ref[pl.ds(at, 2)] = key
-            even, odd = join(out_ref[0, pair, 2:], out_ref[1, pair, 2:])
+            even, odd = join(out_ref[0, pl.ds(pair, 1)], out_ref[1, pl.ds(pair, 1)])
             dq_ref[pl.ds(at, 1)] = even
             dq_ref[pl.ds(at + 1, 1)] = odd
             return carry
@@ -158,6 +160,15 @@
     for axis in ("x", "y"):
         for by in (1, 3):
             pl.semaphore_signal(barrier, inc=1, device_id={axis: step(axis, by)}, device_id_type=MESH)
+    loads = [
+        pltpu.make_async_copy(ref, loaded.at[i], load_sem.at[i])
+        for i, ref in enumerate((q_hbm, k_hbm, v_hbm, g_hbm))
+    ]
+    for load in loads:
+        load.start()
+    for load in loads:
+        load.wait()
+    pack(0)
     pl.semaphore_wait(barrier, ring - 1 + 4)
 
     def columns_of(c):
@@ -171,23 +182,35 @@
         _, z, c = peer_of(offset)
         return remote(mask_ref.at[z], mrecv.at[me], mask_sem.at[offset], {"zl": z, "core": c})
 
-    def in_copy(group, offset):
+    def in_copy(i, offset):
         _, z, c = peer_of(offset)
         return remote(
-            send_ref.at[c, pl.ds(z * rows + group * 2, 2)],
-            ab.at[pl.ds(group * 2, 2), :, columns_of(me)],
-            in_sem.at[group, offset],
+            send_ref.at[c, z * rows + i],
+            ab.at[i, :, columns_of(me)],
+            in_sem.at[i, offset],
             {"zl": z, "core": c},
         )
 
-    def out_copy(group, offset):
+    def slot_of(i, pair):
+        return (rows + i, zls * rows + zl * groups + i) if pair else (i, zl * rows + i)
+
+    def out_copy(i, pair, offset):
         other, z, c = peer_of(offset)
+        source, dest = slot_of(i, pair)
         return remote(
-            obuf.at[group, :, columns_of(other)],
-            out_ref.at[core, zl * groups + group],
-            out_sem.at[group, offset],
+            obuf.at[source, columns_of(other)],
+            out_ref.at[core, dest],
+            out_sem.at[source, offset],
             {"zl": z, "core": c},
         )
+
+    def out_start(i, pair):
+        for offset in range(1, peers):
+            out_copy(i, pair, offset).start()
+
+    def out_keep(i, pair):
+        source, dest = slot_of(i, pair)
+        out_ref[core, dest] = obuf[source, columns_of(me)]
 
     orders = (("x", "y"), ("y", "x"))
 
@@ -200,10 +223,8 @@
     def gather_copy(h, phase, hop, way):
         axis = orders[h][phase]
         by = (1, 3)[way]
-        if hop == 0:
-            ref = block(h, phase, place[axis], None)
-        else:
-            ref = block(h, phase, step(axis, 4 - by), way)
+        half = 1 - way if hop == 1 else way
+        ref = block(h, phase, step(axis, 4 - by) if hop == 2 else place[axis], half)
         return remote(ref, ref, gather_sem.at[h, phase, hop, way], {axis: step(axis, by)})
 
     for offset in range(1, ring):
@@ -213,9 +234,11 @@
         mask_copy(offset).start()
     mrecv[me] = mask_ref[zl]
     for group in range(groups):
-        pack(group)
-        for offset in range(1, peers):
-            in_copy(group, offset).start()
+        if group:
+            pack(group)
+        for i in (group * 2, group * 2 + 1):
+            for offset in range(1, peers):
+                in_copy(i, offset).start()
         ab[group * 2 : group * 2 + 2, :, columns_of(me)] = send_ref[core, pl.ds(zl * rows + group * 2, 2)]
 
     gb[...] = jnp.zeros_like(gb)
@@ -227,13 +250,14 @@
             pieces = [trecv[z * peers + c, h].astype(F32) for c in range(peers)]
             biasb[h, z, place["x"], place["y"]] = jnp.concatenate(pieces, axis=1).astype(BF16)
     for phase in range(2):
-        for h in range(2):
-            for way in range(2):
-                gather_copy(h, phase, 0, way).start()
+        for hop in range(2):
+            for h in range(2):
+                for way in range(2):
+                    gather_copy(h, phase, hop, way).start()
         for h in range(2):
             for way in range(2):
                 gather_copy(h, phase, 0, way).wait_recv()
-                gather_copy(h, phase, 1, way).start()
+                gather_copy(h, phase, 2, way).start()
         if phase == 0:
             for offset in range(1, peers):
                 mask_copy(offset).wait()
@@ -245,6 +269,7 @@
             for way in range(2):
                 gather_copy(h, phase, 0, way).wait_send()
                 gather_copy(h, phase, 1, way).wait()
+                gather_copy(h, phase, 2, way).wait()
 
     def widen(r, carry):
         for h in range(2):
@@ -344,126 +369,142 @@
             last_s.at[lax.rem(spot + offset, ring)], last_r.at[spot], last_sem.at[offset], ring_target(offset)
         )
 
-    def one_group(group, carry):
+    def release(count):
+        def release_row(i, carry):
+            out_start(i, False)
+            return carry
+
+        def release_pair(i, carry):
+            out_start(i, True)
+            return carry
+
+        lax.fori_loop(0, count, release_row, 0)
+        lax.fori_loop(0, groups - 1, release_pair, 0)
+
+    def one_row(i, last):
         for offset in range(1, peers):
-            in_copy(group, offset).wait()
-
-        def prepare(r, carry):
-            i = group * 2 + r
-            a = ab[i, 0].astype(F32)
-            b = ab[i, 1].astype(F32)
-            ar = pltpu.roll(a, 64, 1)
-            br = pltpu.roll(b, 64, 1)
-            for h in range(2):
-                kq[r, h] = jnp.where(lane_head == h, ar, 0.0).astype(BF16)
-                kq[r, 2 + h] = jnp.where(lane_head == 2 + h, ar, 0.0).astype(BF16)
-                vg[r, h] = jnp.where(lane_head == h, br, 0.0).astype(BF16)
-                vg[r, 2 + h] = jnp.where(lane_head == h, b, 0.0).astype(BF16)
-            kt[r] = jnp.transpose(ar).astype(BF16)
-            vk[r] = jnp.zeros_like(vk[r])
-            return carry
-
-        lax.fori_loop(0, 2, prepare, 0)
-
-        def where_of(u):
-            h, ch = u // chunks, lax.rem(u, chunks)
-            return h, pl.ds(pl.multiple_of(ch * chunk, chunk), chunk)
-
-        def scores(r, u):
-            h, cols = where_of(u)
-            i = group * 2 + r
-            s = dot(kq[r, h], ab[i, 0, cols, :], ((1,), (1,)))
+            in_copy(i, offset).wait()
+        if not last:
+            pl.when(i == rows - 2)(lambda: release(rows - 2))
+        a = ab[i, 0].astype(F32)
+        b = ab[i, 1].astype(F32)
+        ar = pltpu.roll(a, 64, 1)
+        br = pltpu.roll(b, 64, 1)
+        for h in range(2):
+            kq[h] = jnp.where(lane_head == h, ar, 0.0).astype(BF16)
+            kq[2 + h] = jnp.where(lane_head == 2 + h, ar, 0.0).astype(BF16)
+            vg[h] = jnp.where(lane_head == h, br, 0.0).astype(BF16)
+            vg[2 + h] = jnp.where(lane_head == h, b, 0.0).astype(BF16)
+        kt[...] = jnp.transpose(ar).astype(BF16)
+        vk[...] = jnp.zeros_like(vk)
+
+        def columns(u):
+            return pl.ds(pl.multiple_of(u * chunk, chunk), chunk)
+
+        def scores(h, u):
+            cols = columns(u)
+            s = dot(kq[h], ab[i, 0, cols, :], ((1,), (1,)))
             top = None
             for k0 in range(0, n, span):
                 m128 = maskf[i, k0 : k0 + span, :]
                 mask = jnp.concatenate([m128] * (chunk // LANES), axis=1) if chunk > LANES else m128[:, :chunk]
                 part = (s[k0 : k0 + span] * SCALE + biasf[h, k0 : k0 + span, cols]) + mask
-                sbuf[r, k0 : k0 + span] = part
+                sbuf[h, k0 : k0 + span] = part
                 part = jnp.max(part.reshape(-1, 8, chunk), axis=0)
                 top = part if top is None else jnp.maximum(top, part)
-            maxbuf[r] = top
-            dpbuf[r] = dot(vg[r, h], ab[i, 1, cols, :], ((1,), (1,)))
-
-        def soft(r, u):
-            h, cols = where_of(u)
-            top = jnp.max(maxbuf[r], axis=0, keepdims=True)
+            maxbuf[h] = top
+            dpbuf[h] = dot(vg[h], ab[i, 1, cols, :], ((1,), (1,)))
+
+        def soft(h, u):
+            cols = columns(u)
+            top = jnp.max(maxbuf[h], axis=0, keepdims=True)
             total = weighted = None
             for k0 in range(0, n, span):
-                e = jnp.exp(sbuf[r, k0 : k0 + span] - top)
-                sbuf[r, k0 : k0 + span] = e
+                e = jnp.exp(sbuf[h, k0 : k0 + span] - top)
+                sbuf[h, k0 : k0 + span] = e
                 first = jnp.sum(e.reshape(-1, 8, chunk), axis=0)
-                second = jnp.sum((e * dpbuf[r, k0 : k0 + span]).reshape(-1, 8, chunk), axis=0)
+                second = jnp.sum((e * dpbuf[h, k0 : k0 + span]).reshape(-1, 8, chunk), axis=0)
                 total = first if total is None else total + first
                 weighted = second if weighted is None else weighted + second
             inverse = 1.0 / jnp.sum(total, axis=0, keepdims=True)
             delta = jnp.sum(weighted, axis=0, keepdims=True) * inverse
             for b in range(8):
                 k0 = b * span
-                p = sbuf[r, k0 : k0 + span] * inverse
-                ds = p * (dpbuf[r, k0 : k0 + span] - delta)
-                pbuf[r, k0 : k0 + span] = p.astype(BF16)
-                lowbuf[r, k0 : k0 + span] = ds.astype(BF16)
+                p = sbuf[h, k0 : k0 + span] * inverse
+                ds = p * (dpbuf[h, k0 : k0 + span] - delta)
+                pbuf[h, k0 : k0 + span] = p.astype(BF16)
+                lowbuf[h, k0 : k0 + span] = ds.astype(BF16)
                 gb[h, b // 4, b % 4, :, :, cols] += ds.reshape(4, tile, chunk)
 
-        def grads(r, u):
-            h, cols = where_of(u)
-            vk[r] += dot(pbuf[r], vg[r, 2 + h, cols, :], ((1,), (0,))) + dot(
-                lowbuf[r], kq[r, 2 + h, cols, :], ((1,), (0,))
+        def grads(h, u):
+            cols = columns(u)
+            vk[...] += dot(pbuf[h], vg[2 + h, cols, :], ((1,), (0,))) + dot(
+                lowbuf[h], kq[2 + h, cols, :], ((1,), (0,))
             )
-            head_rows = kt[r, pl.ds(pl.multiple_of(h * HEAD_DIM, HEAD_DIM), HEAD_DIM), :]
-            at = pl.multiple_of(r * 64 + h * HEAD_DIM, HEAD_DIM)
-            dqt[pl.ds(at, HEAD_DIM), cols] = dot(head_rows, lowbuf[r], ((1,), (0,)))
-
-        steps = 2 * chunks
+            head_rows = kt[h * HEAD_DIM : (h + 1) * HEAD_DIM, :]
+            at = pl.multiple_of(lax.rem(i, 2) * 64 + h * HEAD_DIM, HEAD_DIM)
+            dqt[pl.ds(at, HEAD_DIM), cols] = dot(head_rows, lowbuf[h], ((1,), (0,)))
+
         pbuf[1] = jnp.zeros_like(pbuf[1])
         lowbuf[1] = jnp.zeros_like(lowbuf[1])
         scores(0, 0)
 
         def one_step(u, carry):
             scores(1, u)
-            grads(1, lax.rem(u + steps - 1, steps))
+            grads(1, lax.rem(u + chunks - 1, chunks))
             soft(0, u)
-            scores(0, lax.rem(u + 1, steps))
+            scores(0, lax.rem(u + 1, chunks))
             grads(0, u)
             soft(1, u)
-
-            @pl.when((group == groups - 1) & (u == chunks - 1))
-            def _():
-                sums_begin(0)
-
             return carry
 
-        lax.fori_loop(0, steps, one_step, 0)
-        grads(1, steps - 1)
-
-        def finish(r, carry):
-            obuf[group, r] = (vk[r] * jnp.where(lane_head < 2, 1.0, SCALE)).astype(BF16)
-            return carry
-
-        lax.fori_loop(0, 2, finish, 0)
-        obuf[group, 2] = (jnp.transpose(dqt[...]) * SCALE).astype(BF16)
-        for offset in range(1, peers):
-            out_copy(group, offset).start()
-        out_ref[core, zl * groups + group] = obuf[group, :, columns_of(me)]
+        lax.fori_loop(0, chunks, one_step, 0)
+        if last:
+            sums_begin(0)
+            sums_begin(1)
+        grads(1, chunks - 1)
+        obuf[i] = (vk[...] * jnp.where(lane_head < 2, 1.0, SCALE)).astype(BF16)
+        if last:
+            out_start(i, False)
+        else:
+            pl.when(i == rows - 2)(lambda: out_start(i, False))
+        out_keep(i, False)
+
+    def close_pair(pair):
+        obuf[rows + pair] = (jnp.transpose(dqt[...]) * SCALE).astype(BF16)
+        out_keep(pair, True)
+
+    def early_row(i, carry):
+        one_row(i, False)
+
+        @pl.when(lax.rem(i, 2) == 1)
+        def _():
+            close_pair(i // 2)
+
         return carry
 
-    lax.fori_loop(0, groups, one_group, 0)
-
-    sums_begin(1)
-    for stage in (sums_forward, sums_turn, sums_close, sums_last):
+    lax.fori_loop(0, rows - 1, early_row, 0)
+    one_row(rows - 1, True)
+    sums_forward(0)
+    sums_forward(1)
+    close_pair(groups - 1)
+    for stage in (sums_turn, sums_close, sums_last):
         for h in range(2):
             stage(h)
     for offset in range(1, ring):
         last_copy(offset).start()
+    out_start(groups - 1, True)
     last_r[spot] = last_s[spot]
 
     def drain(group, carry):
         for offset in range(1, peers):
-            out_copy(group, offset).wait()
+            out_copy(group * 2, False, offset).wait()
+            out_copy(group * 2 + 1, False, offset).wait()
+            out_copy(group, True, offset).wait()
         unpack(group)
         return carry
 
-    lax.fori_loop(0, groups, drain, 0)
+    lax.fori_loop(0, groups - 1, drain, 0)
     for offset in range(1, ring):
         last_copy(offset).wait()
     for c in range(cs):
@@ -472,6 +513,7 @@
             for s in range(c + cs, ring, cs):
                 total += last_r[s, h].astype(F32)
             gout_ref[2 * c + h] = total
+    drain(groups - 1, 0)
 
 
 def attention(dims, queries, keys, values, grads, mask, tiles):
@@ -494,11 +536,12 @@
             jax.ShapeDtypeStruct(queries.shape, BF16),
             jax.ShapeDtypeStruct((HEADS, tile, width), F32),
         ),
-        in_specs=[vmem_spec] * 6,
+        in_specs=[pl.BlockSpec(memory_space=pl.ANY)] * 4 + [vmem_spec] * 2,
         out_specs=(vmem_spec,) * 4,
         scratch_shapes=[
+            pltpu.VMEM((4, zls * rows, width, LANES), BF16),
             pltpu.VMEM((cs, zls * rows, 2, width, LANES), BF16),
-            pltpu.VMEM((cs, zls * groups, 3, width, LANES), BF16),
+            pltpu.VMEM((cs, zls * (rows + groups), width, LANES), BF16),
             pltpu.VMEM((2, n, chunk), BF16),
             pltpu.VMEM((2, n, chunk), F32),
             pltpu.VMEM((2, n, chunk), F32),
@@ -511,12 +554,12 @@
             pltpu.VMEM((peers, rows, width), F32),
             pltpu.VMEM((n, rows), F32),
             pltpu.VMEM((rows, n, LANES), F32),
-            pltpu.VMEM((2, 4, n, LANES), BF16),
-            pltpu.VMEM((2, 4, n, LANES), BF16),
-            pltpu.VMEM((2, LANES, n), BF16),
-            pltpu.VMEM((2, n, LANES), F32),
+            pltpu.VMEM((4, n, LANES), BF16),
+            pltpu.VMEM((4, n, LANES), BF16),
+            pltpu.VMEM((LANES, n), BF16),
+            pltpu.VMEM((n, LANES), F32),
             pltpu.VMEM((LANES, n), F32),
-            pltpu.VMEM((groups, 3, n, LANES), BF16),
+            pltpu.VMEM((rows + groups, n, LANES), BF16),
             pltpu.VMEM((ring, 2, tile, width), BF16),
             pltpu.VMEM((2, 2, 4, tile, n), BF16),
             pltpu.VMEM((2, 2, 4, tile, n), BF16),
@@ -529,16 +572,17 @@
             pltpu.VMEM((2, 2, 2, tile, n), BF16),
             pltpu.VMEM((ring, 2, tile, width), BF16),
             pltpu.VMEM((ring, 2, tile, width), BF16),
+            dma((4,)),
             dma((peers, 2)),
-            dma((groups, peers, 2)),
-            dma((groups, peers, 2)),
+            dma((rows, peers, 2)),
+            dma((rows + groups, peers, 2)),
             dma((ring, 2)),
-            dma((2, 2, 2, 2, 2)),
+            dma((2, 2, 3, 2, 2)),
             dma((2, 6, 2, 2)),
             dma((ring, 2)),
         ],
         compiler_params=pltpu.CompilerParams(
-            collective_id=0, has_side_effects=True, vmem_limit_bytes=63 * 1024 * 1024
+            collective_id=0, has_side_effects=True, vmem_limit_bytes=52 * 1024 * 1024
         ),
         cost_estimate=pl.CostEstimate(
             flops=10 * rows * 2 * n * n * LANES, bytes_accessed=32 * 1024 * 1024, transcendentals=0

time: 124 us -> 117 us (0.944)
  Pallas kernels: 117 us -> 112 us
  local copies, waits for them, and re-layouts: 5.31 us -> 3.08 us
    pallas_call x1, Pallas kernels: 117 us -> 112 us  [attention(): pl.pallas_call(functools.partial(kernel, dims), out_shape=(jax.ShapeDtype...]
    unnamed x10 -> x6, local copies, waits for them, and re-layouts: 4.7 us -> 3.07 us
where the time goes in v4:
time: 117 us; the launch traced here: 116 us
  Pallas kernels  112 us (96%)
  local copies, waits for them, and re-layouts  3.08 us (3%)
    pallas_call x1, Pallas kernels, attention(): pl.pallas_call(functools.partial(kernel, dims), out_shape=(jax.ShapeDtype...  112 us
    unnamed x6, local copies, waits for them, and re-layouts  3.07 us

profile of v4, /device:TPU:1, one launch (start us, length us, event | category | flops | bytes accessed | tf_op | source)
XLA Modules:
  0.0 116.4 jit_solution(14797575537302183989)
XLA Ops:
  0.6 0.0 copy-start
  0.6 0.7 add_multiply_fusion
  1.4 0.0 copy-done
  1.4 112.0 %attention_backward.1 = (bf16[24,96,128]{2,1,0:T(8,128)(2,1)S(1)}, bf16[24,96,128]{2,1,0:T(8,128)(2,1)S(1)}, bf16[24,96,128]{2,1,0:T(8,128)(2,1)S(1)}, f32[4,24,96]{2,1,0:T(8,128)S(1)}) custom-call(bf16[24,96,128]{2,1,0:T(8,128)(2,1)} %q_hbm.1, bf16[24,96,128]{2,1,0:T(8,128)(2,1)} %k_hbm.1, bf16[24,96,128]{2,1,0:T(8,128)(2,1)} %v_hbm.1, ...), custom_call_target="tpu_custom_call" | custom-call | flops 9059696640 | bytes 33554432 | tf_op jit(solution)/shard_map/attention_backward/pallas_call | solution.py:531
  113.3 0.8 copy.14
  114.2 0.8 copy.15
  115.0 0.8 copy.16
  115.8 0.6 copy.17
  (1 shorter events, 0.0 us)
Async XLA Ops:
  0.6 0.7 copy-start

commit v5 on v4

--- a/solution.py
+++ b/solution.py
@@ -31,13 +31,14 @@
     k_hbm,
     v_hbm,
     g_hbm,
-    mask_ref,
+    mask_in,
     tile_ref,
     dq_ref,
     dk_ref,
     dv_ref,
     gout_ref,
     loaded,
+    mask_ref,
     send_ref,
     out_ref,
     pbuf,
@@ -166,6 +167,8 @@
     ]
     for load in loads:
         load.start()
+    for z in range(zls):
+        mask_ref[z] = 1000000000.0 * (mask_in[z * rows : (z + 1) * rows].astype(F32) - 1.0)
     for load in loads:
         load.wait()
     pack(0)
@@ -540,6 +543,7 @@
         out_specs=(vmem_spec,) * 4,
         scratch_shapes=[
             pltpu.VMEM((4, zls * rows, width, LANES), BF16),
+            pltpu.VMEM((zls, rows, width), F32),
             pltpu.VMEM((cs, zls * rows, 2, width, LANES), BF16),
             pltpu.VMEM((cs, zls * (rows + groups), width, LANES), BF16),
             pltpu.VMEM((2, n, chunk), BF16),
@@ -591,15 +595,37 @@
     )(queries, keys, values, grads, mask, tiles)
 
 
+def settle_kernel(*refs):
+    count = len(refs) // 2
+    sem = refs[-1]
+    copies = [pltpu.make_async_copy(refs[i], refs[count + i], sem.at[i]) for i in range(count)]
+    for copy in copies:
+        copy.start()
+    for copy in copies:
+        copy.wait()
+
+
+def settle(*arrays):
+    count = len(arrays)
+    return pl.pallas_call(
+        settle_kernel,
+        out_shape=tuple(jax.ShapeDtypeStruct(a.shape, a.dtype) for a in arrays),
+        in_specs=[pl.BlockSpec(memory_space=pltpu.VMEM)] * count,
+        out_specs=(pl.BlockSpec(memory_space=pl.ANY),) * count,
+        scratch_shapes=[pltpu.SemaphoreType.DMA((count,))],
+        compiler_params=pltpu.CompilerParams(vmem_limit_bytes=8 * 1024 * 1024),
+        name="settle",
+    )(*arrays)
+
+
 def local(zhs, zs, cs, query_proj, key_proj, value_proj, pair_bias, pair_mask, grad_out):
-    rows, width, _ = query_proj.shape
+    width = query_proj.shape[1]
     tile = pair_bias.shape[2]
     tiles = jnp.transpose(pair_bias, (0, 2, 1)).reshape(cs, 2, tile, width)
-    mask = 1000000000.0 * (pair_mask.astype(F32) - 1.0)
-    mask = mask.reshape(zs, rows // zs, width)
     grad_query, grad_key, grad_value, gb = attention(
-        (zhs, zs, cs), query_proj, key_proj, value_proj, grad_out, mask, tiles
+        (zhs, zs, cs), query_proj, key_proj, value_proj, grad_out, pair_mask, tiles
     )
+    grad_query, grad_key, grad_value, gb = settle(grad_query, grad_key, grad_value, gb)
     return grad_query, grad_key, grad_value, jnp.transpose(gb, (0, 2, 1))
 
 

time: 117 us -> 115 us (0.983)
  local copies, waits for them, and re-layouts: 3.08 us -> 1.44 us
    unnamed x6 -> x4, local copies, waits for them, and re-layouts: 3.07 us -> 1.44 us
    pallas_call x0 -> x1, Pallas kernels: none -> 1.24 us  [settle(): pl.pallas_call(settle_kernel, out_shape=tuple((jax.ShapeDtypeStruct(a.sha...]
where the time goes in v5:
time: 115 us
  Pallas kernels  113 us (98%)
  local copies, waits for them, and re-layouts  1.44 us (1%)
    pallas_call x1, Pallas kernels, attention(): pl.pallas_call(functools.partial(kernel, dims), out_shape=(jax.ShapeDtype...  112 us

profile of v5, /device:TPU:1, one launch (start us, length us, event | category | flops | bytes accessed | tf_op | source)
XLA Modules:
  0.0 114.9 jit_solution(9099611823743043830)
XLA Ops:
  0.6 0.0 copy-start
  0.6 0.7 copy-done
  1.4 0.0 copy-start.1
  1.4 0.7 copy-done.1
  2.1 111.6 %attention_backward.1 = (bf16[24,96,128]{2,1,0:T(8,128)(2,1)S(1)}, bf16[24,96,128]{2,1,0:T(8,128)(2,1)S(1)}, bf16[24,96,128]{2,1,0:T(8,128)(2,1)S(1)}, f32[4,24,96]{2,1,0:T(8,128)S(1)}) custom-call(bf16[24,96,128]{2,1,0:T(8,128)(2,1)} %q_hbm.1, bf16[24,96,128]{2,1,0:T(8,128)(2,1)} %k_hbm.1, bf16[24,96,128]{2,1,0:T(8,128)(2,1)} %v_hbm.1, ...), custom_call_target="tpu_custom_call" | custom-call | flops 9059696640 | bytes 33554432 | tf_op jit(solution)/shard_map/attention_backward/pallas_call | solution.py:534
  113.7 1.2 %settle.1 = (bf16[24,96,128]{2,1,0:T(8,128)(2,1)}, bf16[24,96,128]{2,1,0:T(8,128)(2,1)}, bf16[24,96,128]{2,1,0:T(8,128)(2,1)}, f32[4,24,96]{2,1,0:T(8,128)}) custom-call(bf16[24,96,128]{2,1,0:T(8,128)(2,1)S(1)} %get-tuple-element.12.refs_0_, bf16[24,96,128]{2,1,0:T(8,128)(2,1)S(1)} %get-tuple-element.13.refs_1_, ...), custom_call_target="tpu_custom_call" | custom-call | tf_op jit(solution)/shard_map/settle/pallas_call | solution.py:610
Async XLA Ops:
  0.6 0.7 copy-start
  1.4 0.7 copy-start.1

commit v6 on v5

--- a/solution.py
+++ b/solution.py
@@ -324,6 +324,9 @@
         for way in range(2):
             first_s[h, way] = terms(h, step(axis, 2), way).astype(BF16)
             first_copy(h, way).start()
+
+    def sums_early(h):
+        axis = orders[h][0]
         for way in range(2):
             second_s[h, way, 1 - way] = terms(h, step(axis, (1, 3)[way]), 1 - way).astype(BF16)
             second_copy(h, way, 1 - way).start()
@@ -465,6 +468,8 @@
         if last:
             sums_begin(0)
             sums_begin(1)
+            sums_early(0)
+            sums_early(1)
         grads(1, chunks - 1)
         obuf[i] = (vk[...] * jnp.where(lane_head < 2, 1.0, SCALE)).astype(BF16)
         if last:

time: 115 us -> 115 us (level)
  no operation moved by 1% of the time
where the time goes in v6:
time: 115 us
  Pallas kernels  113 us (98%)
  local copies, waits for them, and re-layouts  1.44 us (1%)
    pallas_call x1, Pallas kernels, attention(): pl.pallas_call(functools.partial(kernel, dims), out_shape=(jax.ShapeDtype...  112 us

profile of v6, /device:TPU:1, one launch (start us, length us, event | category | flops | bytes accessed | tf_op | source)
XLA Modules:
  0.0 114.9 jit_solution(18270799089585674578)
XLA Ops:
  0.6 0.0 copy-start
  0.6 0.7 copy-done
  1.4 0.0 copy-start.1
  1.4 0.7 copy-done.1
  2.1 111.6 %attention_backward.1 = (bf16[24,96,128]{2,1,0:T(8,128)(2,1)S(1)}, bf16[24,96,128]{2,1,0:T(8,128)(2,1)S(1)}, bf16[24,96,128]{2,1,0:T(8,128)(2,1)S(1)}, f32[4,24,96]{2,1,0:T(8,128)S(1)}) custom-call(bf16[24,96,128]{2,1,0:T(8,128)(2,1)} %q_hbm.1, bf16[24,96,128]{2,1,0:T(8,128)(2,1)} %k_hbm.1, bf16[24,96,128]{2,1,0:T(8,128)(2,1)} %v_hbm.1, ...), custom_call_target="tpu_custom_call" | custom-call | flops 9059696640 | bytes 33554432 | tf_op jit(solution)/shard_map/attention_backward/pallas_call | solution.py:539
  113.7 1.2 %settle.1 = (bf16[24,96,128]{2,1,0:T(8,128)(2,1)}, bf16[24,96,128]{2,1,0:T(8,128)(2,1)}, bf16[24,96,128]{2,1,0:T(8,128)(2,1)}, f32[4,24,96]{2,1,0:T(8,128)}) custom-call(bf16[24,96,128]{2,1,0:T(8,128)(2,1)S(1)} %get-tuple-element.12.refs_0_, bf16[24,96,128]{2,1,0:T(8,128)(2,1)S(1)} %get-tuple-element.13.refs_1_, ...), custom_call_target="tpu_custom_call" | custom-call | tf_op jit(solution)/shard_map/settle/pallas_call | solution.py:615
Async XLA Ops:
  0.6 0.7 copy-start
  1.4 0.7 copy-start.1
